TPU v7x, 32 devices: a whole 2x2x4 slice. The times are simulated.
32 devices in a mesh: band: 8 (over z, x), grid: 4 (over y, core).
Axes of the slice: x: 2, y: 2, z: 4, core: 2. Of those that a mesh axis runs over, the one named last changes fastest.
Arguments:
- partial_density: float32 [8, 128, 128, 128], P('band', 'grid'), may hold values from 0.01 to 1
- node_index: int32 [128, 128, 128], P('grid'), may hold values from 0 to 19
- node_weight: float32 [4, 128, 128, 128], P(None, 'grid'), may hold values from 0 to 1
- node_slope: float32 [4, 128, 128, 128], P(None, 'grid'), may hold values from -6 to 6
- kernel_table: float32 [20, 20, 114], replicated, may hold values from -0.8 to 0.8, as said below
Outputs:
- potential: float32 [128, 128, 128], P('grid')
Inputs may be any that keep to these rules, and one draw needn't show every extreme that they name: node_index(r) is the node at the lower end of the interval of q0 at r; nodes node_index - 1 to node_index + 2 carry the four weights. `kernel_table`: symmetric in its first two indices.
All inputs are finite; a program needn't handle non-finite values.
Results may differ from a plain program's by a relative error of at most 0.0003.
Values sent between devices are 32-bit elements; how exact they have to be, the bound alone decides.
A program may use at most 128 MiB of HBM per device.

v0:
```python
import math

import jax
import jax.numpy as jnp
from jax import lax
from jax.experimental import pallas as pl
from jax.experimental.pallas import tpu as pltpu
from jax.sharding import PartitionSpec as P

def frequency_of(positions, length):
    return jnp.where(positions < length // 2, positions, positions - length)


def shell_split(square_norm):
    root_value = jnp.sqrt(square_norm.astype(jnp.float32))
    shell_idx = root_value.astype(jnp.int32)
    shell_idx = shell_idx - (shell_idx * shell_idx > square_norm).astype(jnp.int32)
    shell_idx = shell_idx + ((shell_idx + 1) * (shell_idx + 1) <= square_norm).astype(jnp.int32)
    fraction = root_value - shell_idx.astype(jnp.float32)
    return (shell_idx, fraction)


def node_fields(count_nodes, intervals, weights):
    node_ids = jnp.arange(count_nodes, dtype=jnp.int32)
    summed = jnp.zeros((count_nodes,) + intervals.shape, jnp.float32)
    for offset in range(4):
        matched = node_ids[:, None, None, None] == (intervals + (offset - 1))[None]
        summed = summed + jnp.where(matched, weights[offset][None], jnp.zeros((), jnp.float32))
    return summed


def phase_table(source_idx, target_idx, modulus):
    product_mod = source_idx[:, None] * target_idx[None, :] % modulus
    angles = product_mod.astype(jnp.float32) * (2.0 * math.pi / modulus)
    return (jnp.cos(angles), jnp.sin(angles))


def contract(pattern, operand, matrix):
    return jnp.einsum(pattern, operand, matrix, precision=lax.Precision.HIGHEST)


def mirrored(values, dim):
    return jnp.roll(jnp.flip(values, dim), 1, dim)


def forward_tables(positions, plane_ids, length):
    cosine, sine = phase_table(positions, plane_ids, length)
    alternating = jnp.where(positions % 2 == 0, 1.0, -1.0).astype(jnp.float32)
    sine = jnp.where(plane_ids[None, :] == 0, -alternating[:, None], sine)
    return (cosine, sine)


def shell_weights_of(square_norm, shell_count):
    shell_ids = jnp.arange(shell_count, dtype=jnp.int32)
    shell_idx, fraction = shell_split(square_norm)
    expand = (slice(None),) + (None,) * square_norm.ndim
    lower_hit = shell_ids[expand] == shell_idx[None]
    upper_hit = shell_ids[expand] == shell_idx[None] + 1
    return jnp.where(lower_hit, 1.0 - fraction[None], 0.0) + jnp.where(
        upper_hit, fraction[None], 0.0
    )


def short(pattern, left, right):
    return jnp.einsum(pattern, left, right, precision=lax.Precision.HIGH)


def halves(values):
    high = values.astype(jnp.bfloat16)
    low = (values - high.astype(jnp.float32)).astype(jnp.bfloat16)
    return high, low


def mix_kernel(count, padded, shell_ref, frac_ref, table_ref, spec_ref, out_ref):
    rows, lanes = shell_ref.shape[1:]
    ids = lax.broadcasted_iota(jnp.int32, (table_ref.shape[1] // 3, lanes), 0)

    def hats(row):
        shell = shell_ref[0, pl.ds(row, 1), :]
        frac = frac_ref[0, pl.ds(row, 1), :]
        return jnp.where(ids == shell, 1.0 - frac, jnp.where(ids == shell + 1, frac, 0.0))

    def step(pair, carry):
        both = jnp.concatenate([hats(2 * pair), hats(2 * pair + 1)], axis=1)
        high, low = halves(both)
        phi = jnp.dot(
            table_ref[...],
            jnp.concatenate([high, high, low], axis=0),
            preferred_element_type=jnp.float32,
        )
        for side in range(2):
            row = 2 * pair + side
            real = jnp.zeros((padded, lanes), jnp.float32)
            imag = jnp.zeros((padded, lanes), jnp.float32)
            for node in range(count):
                part = phi[node * padded : (node + 1) * padded, side * lanes : (side + 1) * lanes]
                real = real + part * spec_ref[0, node, 0, pl.ds(row, 1), :]
                imag = imag + part * spec_ref[1, node, 0, pl.ds(row, 1), :]
            out_ref[0, row, 0] = real[:count]
            out_ref[0, row, 1] = imag[:count]
        return carry

    lax.fori_loop(0, rows // 2, step, 0)


def mix(spectrum, shell, frac, kernel_table):
    _, count, planes, rows, lanes = spectrum.shape
    padded = -(-count // 8) * 8
    depth = -(-(kernel_table.shape[2]) // 128) * 128
    table = jnp.pad(kernel_table, ((0, 0), (0, padded - count), (0, depth - kernel_table.shape[2])))
    table = table.reshape(count * padded, depth)
    rounded = lax.reduce_precision(table, exponent_bits=8, mantissa_bits=7)
    high, low = rounded.astype(jnp.bfloat16), (table - rounded).astype(jnp.bfloat16)
    table = jnp.concatenate([high, low, high], axis=1)
    return pl.pallas_call(
        lambda *refs: mix_kernel(count, padded, *refs),
        grid=(planes,),
        in_specs=[
            pl.BlockSpec((1, rows, lanes), lambda p: (p, 0, 0)),
            pl.BlockSpec((1, rows, lanes), lambda p: (p, 0, 0)),
            pl.BlockSpec(table.shape, lambda p: (0, 0)),
            pl.BlockSpec((2, count, 1, rows, lanes), lambda p: (0, 0, p, 0, 0)),
        ],
        out_specs=pl.BlockSpec((1, rows, 2, count, lanes), lambda p: (p, 0, 0, 0, 0)),
        out_shape=jax.ShapeDtypeStruct((planes, rows, 2, count, lanes), jnp.float32),
    )(shell, frac, table, spectrum)


def per_device(partial_density, node_index, node_weight, node_slope, kernel_table):
    length = node_index.shape[1]
    half = length // 2
    count_nodes = kernel_table.shape[0]
    shell_count = kernel_table.shape[2]
    planes = half // lax.axis_size("band")
    grid_size = lax.axis_size("grid")
    grid_part = length // grid_size
    band_at = lax.axis_index("band")
    grid_at = lax.axis_index("grid")
    full_range = jnp.arange(length, dtype=jnp.int32)
    own_planes = band_at * planes + jnp.arange(planes, dtype=jnp.int32)
    own_rows = grid_at * grid_part + jnp.arange(grid_part, dtype=jnp.int32)
    lower = ((full_range >= 1) & (full_range < half)).astype(jnp.float32)
    upper = (full_range > half).astype(jnp.float32)
    single = 1.0 - lower - upper
    joint = (own_planes == 0)[:, None, None, None, None]
    cosine, sine = phase_table(full_range, full_range, length)
    forward = jnp.stack(
        [jnp.stack([cosine, -sine], 1), jnp.stack([sine, cosine], 1)]
    )
    low_only = lower + single
    packed = jnp.stack(
        [
            jnp.stack([cosine * low_only, -sine * lower], 1),
            jnp.stack([cosine * upper, -sine * upper + cosine * single], 1),
        ]
    )
    forward_y = jnp.where(joint, packed[None], forward[None])
    backward = jnp.stack(
        [jnp.stack([cosine, sine], 1), jnp.stack([-sine, cosine], 1)]
    )
    lower_col, upper_col, single_col = (v[:, None] for v in (lower, upper, single))
    opened = jnp.stack(
        [
            jnp.stack([cosine * (2.0 * lower_col + single_col), cosine * (2.0 * upper_col)], 1),
            jnp.stack(
                [sine * (-2.0 * lower_col), sine * (-2.0 * upper_col) + cosine * single_col], 1
            ),
        ]
    )
    backward_y = jnp.where(joint, opened[None], backward[None])

    density = lax.psum(partial_density[0], "band")
    theta_fields = density[None] * node_fields(count_nodes, node_index, node_weight)
    cosine_z, sine_z = forward_tables(full_range, own_planes, length)
    table_z = jnp.stack([cosine_z, -sine_z], 1)
    columns = short("zcp,axyz->cpaxy", table_z, theta_fields)
    waves = short("cpaxy,pcydw->wdapx", columns, forward_y)
    waves = waves.reshape((grid_size, grid_part) + waves.shape[1:])
    pencils = lax.all_to_all(waves, "grid", split_axis=0, concat_axis=0, tiled=True)
    forward_x = forward.reshape((2, grid_size, grid_part) + forward.shape[2:])
    spectrum = short("gwdapx,dgxev->eapwv", pencils, forward_x)

    freq_x = frequency_of(full_range, length)
    square_x = freq_x * freq_x
    freq_rows = frequency_of(own_rows, length)
    square_rows = freq_rows * freq_rows
    third_square = jnp.where(
        (own_planes[:, None] == 0) & (own_rows[None, :] > half),
        half * half,
        (own_planes * own_planes)[:, None],
    )
    square_norm = (third_square + square_rows[None, :])[:, :, None] + square_x
    shell, frac = shell_split(square_norm)
    mixed = mix(spectrum, shell, frac, kernel_table)

    flag = ((own_rows[0] == 0) | (own_rows[0] == half)) & (own_planes[0] == 0)
    first_norm = square_x + square_rows[0]
    pair_norm = jnp.stack([first_norm, first_norm + half * half])
    kernels = contract("abs,sqx->qabx", kernel_table, shell_weights_of(pair_norm, shell_count))
    spread = (0.5 * flag.astype(jnp.float32)) * (kernels[0] - kernels[1])
    base = spectrum[:, :, 0, 0, :]
    turned = mirrored(base, 2)
    delta = jnp.stack([turned[0] - base[0], -turned[1] - base[1]])
    extra = jnp.sum(spread[None] * delta[:, :, None, :], axis=1)
    mixed = mixed.at[0, 0].add(extra)

    backward_x = backward.reshape(2, length, 2, grid_size, grid_part)
    inverse = short("pwdbv,dvegx->gwebpx", mixed, backward_x)
    returned = lax.all_to_all(inverse, "grid", split_axis=0, concat_axis=0, tiled=True)
    backward_y = backward_y.reshape((planes, 2, grid_size, grid_part, 2, length))
    slab = short("gwdbpx,pdgwcy->cpbxy", returned, backward_y)
    cosine_own, sine_own = phase_table(own_planes, full_range, length)
    alternating = jnp.where(full_range % 2 == 0, 1.0, -1.0).astype(jnp.float32)
    cosine_back = jnp.where(own_planes[:, None] == 0, 1.0, 2.0 * cosine_own)
    sine_back = jnp.where(own_planes[:, None] == 0, -alternating[None, :], 2.0 * sine_own)
    table_back = jnp.stack([cosine_back, -sine_back]) * (1.0 / float(length) ** 3)
    field_parts = short("cpbxy,cpz->bxyz", slab, table_back)
    slopes = node_fields(count_nodes, node_index, node_slope)
    partial_potential = jnp.sum(field_parts * slopes, axis=0)
    return lax.psum(partial_potential, "band")


def solution(mesh):
    placed = (
        P("band", "grid", None, None),
        P("grid", None, None),
        P(None, "grid", None, None),
        P(None, "grid", None, None),
        P(),
    )
    return jax.shard_map(
        per_device, mesh=mesh, in_specs=placed, out_specs=P("grid", None, None), check_vma=False
    )
```

profile of v0, /device:TPU:1, one launch (start us, length us, event | category | flops | bytes accessed | tf_op | source)
XLA Modules:
  0.0 749.5 jit_solution(15653981110565317054)
XLA Ops:
  12.5 3.5 slice_bitcast_fusion.7
  16.0 98.9 %all-reduce.4.cloned.1.call-done = f32[32,128,128]{2,1,0:T(8,128)} async-done(((f32[32,128,128]{2,1,0:T(8,128)}), f32[32,128,128]{2,1,0:T(8,128)}) %all-reduce.4.cloned.1.call-update) | async-done | bytes 2097168 | tf_op jit(solution)/shard_map/psum | solution.py:172
  115.0 35.8 %fusion.39 = f32[2,8,20,32,128,1]{4,1,3,2,0,5:T(8,128)S(1)} fusion(f32[32,128,128]{2,1,0:T(8,128)} %get-tuple-element.22, s32[32,128,128]{2,1,0:T(8,128)} %get-tuple-element.31, f32[32,128,128]{2,1,0:T(8,128)} %get-tuple-element.23, s32[32,128,128]{2,1,0:T(8,128)} %get-tuple-element.32, f32[32,128,128]{2,1,0:T(8,128)} %get-tuple-element.21, ...), kind=kOutput, calls=%fused_computation.39 | convolution fusion | flops 1132464128 | bytes 24125440 | tf_op jit(solution)/shard_map/zcp,axyz->cpaxy/dot_general | solution.py:65
  150.8 5.0 fusion.30
  155.7 15.4 %reshape.1184 = f32[4,32,2,20,8,32]{1,0,5,3,2,4:T(4,128)} reshape(f32[128,2,20,8,32]{0,4,2,1,3:T(8,128)} %fusion.30) | data formatting | bytes 10485760 | tf_op jit(solution)/shard_map/reshape | solution.py:178
  171.2 24.0 %copy.26 = f32[4,32,2,20,8,32]{5,1,2,4,3,0:T(8,128)} copy(f32[4,32,2,20,8,32]{1,0,5,3,2,4:T(4,128)} %reshape.1184) | data formatting | bytes 10485760 | tf_op jit(solution)/shard_map/reshape | solution.py:178
  195.1 23.5 %reshape.1204 = f32[4,1,327680]{2,1,0:T(1,128)} reshape(f32[4,20,8,2,32,32]{5,4,3,2,1,0:T(8,128)} %bitcast.148) | data formatting | bytes 10485760
  218.6 17.0 %all-to-all-start = ((f32[4,1,327680]{2,1,0:T(1,128)}), f32[4,1,327680]{2,1,0:T(1,128)}, u32[]{:S(2)}, u32[]{:S(2)}) async-start(f32[4,1,327680]{2,1,0:T(1,128)} %reshape.1204), calls=%async_computation | async-start | bytes 10485760 | tf_op jit(solution)/shard_map/all_to_all | solution.py:179
  239.9 54.2 %all-to-all-done = f32[4,1,327680]{2,1,0:T(1,128)} async-done(((f32[4,1,327680]{2,1,0:T(1,128)}), f32[4,1,327680]{2,1,0:T(1,128)}, u32[]{:S(2)}, u32[]{:S(2)}) %all-to-all-start) | async-done | bytes 5242912 | tf_op jit(solution)/shard_map/all_to_all | solution.py:179
  294.6 17.9 %reduce.2 = f32[4,327680]{1,0:T(4,128)} reduce(f32[4,1,327680]{2,1,0:T(1,128)} %all-to-all-done, f32[]{:T(128)} %broadcast.1674), dimensions={1}, to_apply=%all_to_all.6.reduce_sub_computation | reduce | bytes 10485764 | tf_op jit(solution)/shard_map/all_to_all | solution.py:179
  312.5 16.7 %reshape.1205 = f32[4,20,8,2,32,32]{5,4,3,2,1,0:T(8,128)} reshape(f32[4,327680]{1,0:T(4,128)} %reduce.2) | data formatting | bytes 10485760
  329.2 16.0 %fusion.33.refs_3_ = f32[2,20,8,32,128]{4,3,2,1,0:T(8,128)S(1)} fusion(f32[1,4,32,1,128]{4,2,1,0,3:T(8,128)S(1)} %get-tuple-element.43, f32[1,4,32,1,128]{4,2,1,0,3:T(8,128)S(1)} %get-tuple-element.40, f32[1,4,32,1,128]{4,2,1,0,3:T(8,128)S(1)} %get-tuple-element.42, f32[4,20,8,2,32,32]{5,4,3,2,1,0:T(8,128)} %reshape.1205), kind=kOutput, calls=%fused_computation.37 | convolution fusion | flops 2013462528 | bytes 10682368 | tf_op jit(solution)/shard_map/gwdapx,dgxev->eapwv/dot_general | solution.py:65
  349.1 40.6 %shard_map.55 = f32[8,32,2,20,128]{4,3,2,1,0:T(8,128)} custom-call(s32[8,32,128]{2,1,0:T(8,128)} %convert_add_fusion.refs_0_, f32[8,32,128]{2,1,0:T(8,128)} %fusion.64.refs_1_, bf16[480,384]{1,0:T(8,128)(2,1)} %pad_maximum_fusion.refs_2_, f32[2,20,8,32,128]{4,3,2,1,0:T(8,128)} %copy-done.2), custom_call_target="tpu_custom_call" | custom-call | tf_op jit(solution)/shard_map/pallas_call | solution.py:115
  391.0 13.3 %convolution_bitcast_fusion = f32[4,32,2,20,8,32]{1,5,3,4,0,2:T(8,128)} fusion(f32[8,32,2,20,128,1,1]{4,3,2,1,0,6,5:T(8,128)} %bitcast.149, f32[1,128,1,4,32]{1,4,3,2,0:T(8,128)S(1)} %get-tuple-element.45, f32[1,128,1,4,32]{1,4,3,2,0:T(8,128)S(1)} %get-tuple-element.46, f32[1,128,1,4,32]{1,4,3,2,0:T(8,128)S(1)} %get-tuple-element.44), kind=kOutput, calls=%fused_computation.31 | convolution fusion | flops 2013462528 | bytes 10682368 | tf_op jit(solution)/shard_map/pwdbv,dvegx->gwebpx/dot_general | solution.py:65
  404.3 20.8 %copy.33 = f32[4,32,2,20,8,32]{5,4,3,2,1,0:T(8,128)} copy(f32[4,32,2,20,8,32]{1,5,3,4,0,2:T(8,128)} %convolution_bitcast_fusion) | data formatting | bytes 10485760 | tf_op jit(solution)/shard_map/pwdbv,dvegx->gwebpx/transpose | solution.py:65
  425.1 23.5 %reshape.1206 = f32[4,1,327680]{2,1,0:T(1,128)} reshape(f32[4,32,2,20,8,32]{5,4,3,2,1,0:T(8,128)} %copy.33) | data formatting | bytes 10485760
  448.6 6.1 all-to-all-start.1
  454.9 7.1 slice_bitcast_fusion.3
  462.0 51.2 %all-to-all-done.1 = f32[4,1,327680]{2,1,0:T(1,128)} async-done(((f32[4,1,327680]{2,1,0:T(1,128)}), f32[4,1,327680]{2,1,0:T(1,128)}, u32[]{:S(2)}, u32[]{:S(2)}) %all-to-all-start.1) | async-done | bytes 5242912 | tf_op jit(solution)/shard_map/all_to_all | solution.py:209
  513.2 18.0 %reduce.3 = f32[4,327680]{1,0:T(4,128)} reduce(f32[4,1,327680]{2,1,0:T(1,128)} %all-to-all-done.1, f32[]{:T(128)} %broadcast.1674), dimensions={1}, to_apply=%all_to_all.7.reduce_sub_computation | reduce | bytes 10485764 | tf_op jit(solution)/shard_map/all_to_all | solution.py:209
  531.3 16.7 %reshape.1207 = f32[4,32,2,20,8,32]{5,4,3,2,1,0:T(8,128)} reshape(f32[4,327680]{1,0:T(4,128)} %reduce.3) | data formatting | bytes 10485760
  548.0 34.4 %fusion.36 = f32[2,8,20,32,128]{4,3,2,0,1:T(8,128)} fusion(f32[4,32,2,20,8,32,1]{5,4,3,2,1,0,6:T(8,128)} %bitcast.147, f32[2,4,32,2,128]{4,2,1,0,3:T(8,128)S(1)} %get-tuple-element.61, f32[2,4,32,2,128]{4,2,1,0,3:T(8,128)S(1)} %get-tuple-element.62, pred[8]{0:T(512)(128)(4,1)S(1)} %broadcast_compare_fusion.1), kind=kOutput, calls=%fused_computation.38 | convolution fusion | flops 2013790208 | bytes 11010056 | tf_op jit(solution)/shard_map/gwdbpx,pdgwcy->cpbxy/dot_general | solution.py:65
  582.4 56.2 %fusion = f32[32,128,128]{2,1,0:T(8,128)} fusion(f32[32,128,128]{2,1,0:T(8,128)} %get-tuple-element.26, f32[32,128,128]{2,1,0:T(8,128)} %get-tuple-element.27, f32[32,128,128]{2,1,0:T(8,128)} %get-tuple-element.25, f32[32,128,128]{2,1,0:T(8,128)} %get-tuple-element.24, s32[32,128,128]{2,1,0:T(8,128)} %get-tuple-element.31, ...), kind=kOutput, calls=%fused_computation.1 | convolution fusion | flops 1142423552 | bytes 24125440 | tf_op jit(solution)/shard_map/cpbxy,cpz->bxyz/dot_general | solution.py:65
  638.7 100.7 %all-reduce.6.cloned.1.call-done = f32[32,128,128]{2,1,0:T(8,128)} async-done(((f32[32,128,128]{2,1,0:T(8,128)}), f32[32,128,128]{2,1,0:T(8,128)}) %all-reduce.6.cloned.1.call-update) | async-done | bytes 2097168 | tf_op jit(solution)/shard_map/psum | solution.py:220
  (71 shorter events, 18.9 us)
Async XLA Ops:
  6.5 2.2 copy-start
  6.5 108.4 %all-reduce.4.cloned.1.call-start = ((), (), s32[]{:S(2)}) async-start(), calls=%async_computation.2 | async-start | bytes 4194304 | tf_op jit(solution)/shard_map/psum | solution.py:172
  7.3 5.2 copy-start.3
  7.3 8.7 %copy-start.5 = (f32[128]{0:T(128)}, f32[128]{0:T(128)S(1)}, u32[]{:S(2)}) copy-start(f32[128]{0:T(128)S(1)} %fusion.134) | copy-start | bytes 1540
  218.6 17.1 %copy-start.4 = (f32[20,20,114]{2,1,0:T(8,128)S(1)}, f32[20,20,114]{2,1,0:T(8,128)}, u32[]{:S(2)}) copy-start(f32[20,20,114]{2,1,0:T(8,128)} %param.11) | copy-start | bytes 547204
  218.6 75.5 %all-to-all-start = ((f32[4,1,327680]{2,1,0:T(1,128)}), f32[4,1,327680]{2,1,0:T(1,128)}, u32[]{:S(2)}, u32[]{:S(2)}) async-start(f32[4,1,327680]{2,1,0:T(1,128)} %reshape.1204), calls=%async_computation | async-start | bytes 10485760 | tf_op jit(solution)/shard_map/all_to_all | solution.py:179
  345.2 2.3 copy-start.2
  448.6 6.1 copy-start.6
  448.6 64.6 %all-to-all-start.1 = ((f32[4,1,327680]{2,1,0:T(1,128)}), f32[4,1,327680]{2,1,0:T(1,128)}, u32[]{:S(2)}, u32[]{:S(2)}) async-start(f32[4,1,327680]{2,1,0:T(1,128)} %reshape.1206), calls=%async_computation.1 | async-start | bytes 10485760 | tf_op jit(solution)/shard_map/all_to_all | solution.py:209
  454.7 284.6 %all-reduce.6.cloned.1.call-start = ((), (), s32[]{:S(2)}) async-start(), calls=%async_computation.3 | async-start | bytes 4194304 | tf_op jit(solution)/shard_map/psum | solution.py:220
  548.0 34.4 %copy-start.1 = (s32[32,128,128]{2,1,0:T(8,128)S(1)}, s32[32,128,128]{2,1,0:T(8,128)}, u32[]{:S(2)}) copy-start(s32[32,128,128]{2,1,0:T(8,128)} %get-tuple-element.30) | copy-start | bytes 6291460
Sparse Core Ops, SparseCore 0:
  11.0 103.9 all-reduce.3
  638.8 100.5 all-reduce.5
where the time goes:
time: 761 us; the launch traced here: 750 us
  waiting for transfers between devices  306 us (40%)
  matrix products  161 us (21%)
  local copies, waits for them, and re-layouts  158 us (21%)
  other arithmetic  46.6 us (6%)
  Pallas kernels  40.6 us (5%)
  starting transfers between devices  23.1 us (3%)
  between operations  14 us (2%)
    dot_general x6, matrix products, short(): return jnp.einsum(pattern, left, right, precision=lax.Precision.HIGH)  161 us
    psum x1, waiting for transfers between devices, per_device(): return lax.psum(partial_potential, 'band')  101 us
    psum x1, waiting for transfers between devices, per_device(): density = lax.psum(partial_density[0], 'band')  98.9 us
    unnamed x20, local copies, waits for them, and re-layouts  86.5 us
    all_to_all x1, waiting for transfers between devices, per_device(): lax.all_to_all(waves, 'grid', split_axis=0, concat_axis=0, tiled=True)  54.2 us
    all_to_all x1, waiting for transfers between devices, per_device(): lax.all_to_all(inverse, 'grid', split_axis=0, concat_axis=0, tiled=True)  51.2 us
    pallas_call x1, Pallas kernels, mix(): pl.pallas_call(lambda *refs: mix_kernel(count, padded, *refs), grid=(plan...  40.6 us
    reshape x2, local copies, waits for them, and re-layouts, per_device(): waves = waves.reshape((grid_size, grid_part) + waves.shape[1:])  39.4 us
  transfers between devices with their start and end apart: 4, of which 4 were waited for; matrix products, arithmetic and copies ran while one was open for 3% of the time, Pallas kernels for 0%

commit v1 on v0

--- a/solution.py
+++ b/solution.py
@@ -2,6 +2,7 @@
 
 import jax
 import jax.numpy as jnp
+import numpy as np
 from jax import lax
 from jax.experimental import pallas as pl
 from jax.experimental.pallas import tpu as pltpu
@@ -220,6 +221,638 @@
     return lax.psum(partial_potential, "band")
 
 
+LANES = 128
+SUBLANES = 8
+MESH = pl.DeviceIdType.MESH
+VMEM = pltpu.VMEM
+
+
+def split_table(table):
+    high = np.asarray(table).astype(jnp.bfloat16)
+    low = (np.asarray(table) - high.astype(np.float64)).astype(jnp.bfloat16)
+    return high, low
+
+
+def angles_of(sources, targets, length):
+    phase = (np.outer(sources, targets) % length) * (2.0 * np.pi / length)
+    return np.cos(phase), np.sin(phase)
+
+
+def complex_table(cosine, sine):
+    return np.stack([np.stack([cosine, -sine], 1), np.stack([sine, cosine], 1)])
+
+
+def constant_tables(length, bands, planes):
+    points = np.arange(length)
+    half = length // 2
+    cosine, sine = angles_of(points, points, length)
+    lower = ((points >= 1) & (points < half)).astype(np.float64)
+    upper = (points > half).astype(np.float64)
+    single = 1.0 - lower - upper
+    forward = complex_table(cosine, sine)
+    backward = complex_table(cosine, -sine)
+    packed = np.stack(
+        [
+            np.stack([cosine * (lower + single), -sine * lower], 1),
+            np.stack([cosine * upper, -sine * upper + cosine * single], 1),
+        ]
+    )
+    lo, up, one = (v[:, None] for v in (lower, upper, single))
+    opened = np.stack(
+        [
+            np.stack([cosine * (2 * lo + one), cosine * (2 * up)], 1),
+            np.stack([sine * (-2 * lo), sine * (-2 * up) + cosine * one], 1),
+        ]
+    )
+    square = (2 * length, 2 * length)
+
+    def right(table):
+        high, low = split_table(table.reshape(square))
+        return np.concatenate([high, high, low], 0)
+
+    def left(table):
+        high, low = split_table(table.reshape(square).T)
+        return np.concatenate([high, low, high], 1)
+
+    alternating = np.where(points % 2 == 0, 1.0, -1.0)
+    z_forward, z_backward = [], []
+    for band in range(bands):
+        ids = band * planes + np.arange(planes)
+        cos_z, sin_z = angles_of(ids, points, length)
+        minus = np.where(ids[:, None] == 0, alternating[None], -sin_z)
+        rows = np.concatenate([cos_z, minus], 0)
+        high, low = split_table(rows)
+        top = np.concatenate([high, high], 1)
+        bottom = np.concatenate([low, np.zeros_like(low)], 1)
+        z_forward.append(np.concatenate([top, bottom], 0))
+        first = ids[:, None] == 0
+        rows = np.concatenate(
+            [np.where(first, 1.0, 2.0 * cos_z), np.where(first, alternating[None], -2.0 * sin_z)]
+        ) / float(length) ** 3
+        high, low = split_table(rows.T)
+        z_backward.append(np.concatenate([high, low, high], 1))
+    return {
+        "y_forward": np.stack([right(packed), right(forward)]),
+        "y_backward": np.stack([right(opened), right(backward)]),
+        "x_forward": left(forward),
+        "x_backward": left(backward),
+        "z_forward": np.stack(z_forward),
+        "z_backward": np.stack(z_backward),
+    }
+
+
+def triple_left(values):
+    high, low = halves(values)
+    return jnp.concatenate([high, low, high], axis=1)
+
+
+def triple_right(values):
+    high, low = halves(values)
+    return jnp.concatenate([high, high, low], axis=0)
+
+
+def matmul(left, right):
+    return jnp.dot(left, right, preferred_element_type=jnp.float32)
+
+
+def matmul_nt(left, right):
+    return lax.dot_general(
+        left, right, (((1,), (1,)), ((), ())), preferred_element_type=jnp.float32
+    )
+
+
+def matmul_tn(left, right):
+    return lax.dot_general(
+        left, right, (((0,), (0,)), ((), ())), preferred_element_type=jnp.float32
+    )
+
+
+def greet(axis, targets):
+    barrier = pltpu.get_barrier_semaphore()
+    for target in targets:
+        pl.semaphore_signal(barrier, inc=1, device_id={axis: target}, device_id_type=MESH)
+    pl.semaphore_wait(barrier, len(targets))
+
+
+def sum_kernel(outer, in_ref, out_ref, near_buf, stage, far_buf, sems):
+    me = lax.axis_index("band")
+    far, near = me // 2, lax.rem(me, 2)
+    partner = far * 2 + (1 - near)
+    others = [lax.rem(far + 1 + j, outer) for j in range(outer)]
+    back = [lax.rem(far + outer - 1 - j, outer) for j in range(outer)]
+    rows = in_ref.shape[0] // 2
+    part = rows // outer
+    greet("band", [partner] + [o * 2 + near for o in others[:-1]])
+
+    def piece(side, quarter):
+        return pl.ds(side * rows + quarter * part, part)
+
+    def remote(src, dst, row, j, target):
+        return pltpu.make_async_remote_copy(
+            src_ref=src,
+            dst_ref=dst,
+            send_sem=sems.at[row, 0, j],
+            recv_sem=sems.at[row, 1, j],
+            device_id={"band": target},
+            device_id_type=MESH,
+        )
+
+    near_copies = [
+        remote(in_ref.at[piece(1 - near, others[j])], near_buf.at[j], 0, j, partner)
+        for j in range(outer)
+    ]
+    for copy in near_copies:
+        copy.start()
+    far_copies = []
+    for j in range(outer - 1):
+        near_copies[j].wait_recv()
+        stage[j] = in_ref[piece(near, others[j])] + near_buf[j]
+        copy = remote(stage.at[j], far_buf.at[j], 1, j, others[j] * 2 + near)
+        copy.start()
+        far_copies.append(copy)
+    near_copies[outer - 1].wait_recv()
+    total = in_ref[piece(near, far)] + near_buf[outer - 1]
+    for copy in far_copies:
+        copy.wait_recv()
+    for j in range(outer - 1):
+        total = total + far_buf[j]
+    own = piece(near, far)
+    out_ref[own] = total
+    gathers = []
+    for j in range(outer - 1):
+        copy = remote(out_ref.at[own], out_ref.at[own], 2, j, others[j] * 2 + near)
+        copy.start()
+        gathers.append(copy)
+    passes = [remote(out_ref.at[own], out_ref.at[own], 3, outer - 1, partner)]
+    passes[0].start()
+    for j in range(outer - 1):
+        gathers[j].wait_recv()
+        block = out_ref.at[piece(near, back[j])]
+        copy = remote(block, block, 3, j, partner)
+        copy.start()
+        passes.append(copy)
+    for copy in passes:
+        copy.wait_recv()
+    for copy in near_copies + far_copies + gathers + passes:
+        copy.wait_send()
+
+
+def band_sum(values, collective_id):
+    outer = lax.axis_size("band") // 2
+    part = values.shape[0] // (2 * outer)
+    piece = (part,) + values.shape[1:]
+    return pl.pallas_call(
+        lambda *refs: sum_kernel(outer, *refs),
+        in_specs=[pl.BlockSpec(memory_space=VMEM)],
+        out_specs=pl.BlockSpec(memory_space=VMEM),
+        out_shape=jax.ShapeDtypeStruct(values.shape, jnp.float32),
+        scratch_shapes=[
+            VMEM((outer,) + piece, jnp.float32),
+            VMEM((outer - 1,) + piece, jnp.float32),
+            VMEM((outer - 1,) + piece, jnp.float32),
+            pltpu.SemaphoreType.DMA((4, 2, outer)),
+        ],
+        compiler_params=pltpu.CompilerParams(
+            collective_id=collective_id, has_side_effects=True, vmem_limit_bytes=60 * 2**20
+        ),
+    )(values)
+
+
+def forward_kernel(
+    sizes, density_ref, index_ref, weight_ref, tz_ref, ty_ref, out_ref, theta, columns, send, sems
+):
+    count, grid_size, steps, planes, length = sizes
+    step_rows = SUBLANES * length
+    band_at, me = lax.axis_index("band"), lax.axis_index("grid")
+    order = [lax.rem(me + 1 + j, grid_size) for j in range(grid_size)]
+    per = planes // grid_size
+    rows = count * SUBLANES
+    greet("grid", order[:-1])
+
+    def copy_of(step, slot, j):
+        return pltpu.make_async_remote_copy(
+            src_ref=send.at[slot, j],
+            dst_ref=out_ref.at[:, :, me * steps + step],
+            send_sem=sems.at[0, step, j],
+            recv_sem=sems.at[1, step, j],
+            device_id={"grid": order[j]},
+            device_id_type=MESH,
+        )
+
+    def fill(step):
+        block = 32
+
+        def body(at, carry):
+            x_at = step * SUBLANES + at // (length // block)
+            start = pl.multiple_of(lax.rem(at, length // block) * block, block)
+            place = pl.ds(pl.multiple_of(at * block, block), block)
+            index = index_ref[x_at, pl.ds(start, block), :] - 1
+            amount = density_ref[x_at, pl.ds(start, block), :]
+            parts = [amount * weight_ref[j, x_at, pl.ds(start, block), :] for j in range(4)]
+            for node in range(count):
+                value = jnp.where(index == node, parts[0], 0.0)
+                for j in range(1, 4):
+                    value = jnp.where(index == node - j, parts[j], value)
+                high, low = halves(value)
+                theta[node, place, 0:length] = high
+                theta[node, place, length : 2 * length] = low
+            return carry
+
+        lax.fori_loop(0, step_rows // block, body, 0)
+
+    def columns_of(step):
+        table = tz_ref[band_at]
+
+        def body(node, carry):
+            for pair in range(SUBLANES // 2):
+                block = theta[node, pair * 2 * length : (pair + 1) * 2 * length, :]
+                out = matmul_nt(table, block)
+                out = out[: 2 * planes] + out[2 * planes :]
+                for side in range(2):
+                    for c in range(2):
+                        row = c * planes * rows + node * SUBLANES + pair * 2 + side
+                        columns[pl.ds(row, planes, stride=rows), :] = out[
+                            c * planes : (c + 1) * planes, side * length : (side + 1) * length
+                        ]
+            return carry
+
+        lax.fori_loop(0, count, body, 0)
+
+    def waves_of(step, slot, j):
+        for k in range(per):
+            plane = order[j] * per + k
+            start = pl.multiple_of(plane * rows, rows)
+            left = jnp.concatenate(
+                [columns[pl.ds(c * planes * rows + start, rows), :] for c in range(2)], axis=1
+            )
+            kind = jnp.minimum(plane + band_at * planes, 1)
+            out = matmul(triple_left(left), ty_ref[kind])
+            for d in range(2):
+                value = out[:, d * length : (d + 1) * length]
+                if j < grid_size - 1:
+                    send[slot, j, k, d] = value
+                else:
+                    out_ref[k, d, me * steps + step] = value
+
+    for step in range(steps):
+        slot = step % 2
+        fill(step)
+        columns_of(step)
+        for j in range(grid_size):
+            if step >= 2 and j < grid_size - 1:
+                copy_of(step - 2, slot, j).wait_send()
+            waves_of(step, slot, j)
+            if j < grid_size - 1:
+                copy_of(step, slot, j).start()
+    for step in range(steps):
+        for j in range(grid_size - 1):
+            if step >= steps - 2:
+                copy_of(step, step % 2, j).wait_send()
+            copy_of(step, step % 2, j).wait_recv()
+
+
+def forward(density, node_index, node_weight, tables, count, planes, grid_size):
+    grid_part, length = density.shape[:2]
+    steps = grid_part // SUBLANES
+    per = planes // grid_size
+    sizes = (count, grid_size, steps, planes, length)
+    rows = count * SUBLANES
+    return pl.pallas_call(
+        lambda *refs: forward_kernel(sizes, *refs),
+        in_specs=[pl.BlockSpec(memory_space=VMEM)] * 5,
+        out_specs=pl.BlockSpec(memory_space=VMEM),
+        out_shape=jax.ShapeDtypeStruct(
+            (per, 2, grid_size * steps, rows, length), jnp.float32
+        ),
+        scratch_shapes=[
+            VMEM((count, SUBLANES * length, 2 * length), jnp.bfloat16),
+            VMEM((2 * planes * rows, length), jnp.float32),
+            VMEM((2, grid_size - 1, per, 2, rows, length), jnp.float32),
+            pltpu.SemaphoreType.DMA((2, steps, grid_size - 1)),
+        ],
+        compiler_params=pltpu.CompilerParams(
+            collective_id=1, has_side_effects=True, vmem_limit_bytes=60 * 2**20
+        ),
+    )(density, node_index, node_weight, tables["z_forward"], tables["y_forward"])
+
+
+def middle_kernel(
+    sizes,
+    waves_ref,
+    shell_ref,
+    frac_ref,
+    pair_shell_ref,
+    pair_frac_ref,
+    table_ref,
+    tx_ref,
+    ti_ref,
+    out_ref,
+    spec,
+    mixed,
+    phi,
+    extra,
+    send,
+    sems,
+):
+    count, padded, grid_size, planes, length, group = sizes
+    per = planes // grid_size
+    grid_part = length // grid_size
+    wide = per * length
+    half = length // 2
+    band_at, me = lax.axis_index("band"), lax.axis_index("grid")
+    order = [lax.rem(me + 1 + j, grid_size) for j in range(grid_size)]
+    joint = (band_at == 0) & (me == 0)
+    greet("grid", order[:-1])
+
+    lane = lax.broadcasted_iota(jnp.int32, (16, wide), 1)
+    slot = lax.broadcasted_iota(jnp.int32, (16, wide), 0)
+    chosen = jnp.where(lane == slot * half, 1.0, 0.0)
+    chosen = jnp.where(slot < 2, chosen, 0.0).astype(jnp.bfloat16)
+
+    def block_of(node, d):
+        parts = [
+            waves_ref[k, d, :, pl.ds(pl.multiple_of(node * SUBLANES, SUBLANES), SUBLANES), :]
+            for k in range(per)
+        ]
+        return jnp.concatenate([p.reshape(length, length) for p in parts], axis=1)
+
+    def to_spectrum(node, carry):
+        values = jnp.concatenate([block_of(node, 0), block_of(node, 1)], axis=0)
+        spec[node] = matmul(tx_ref[...], triple_right(values))
+        return carry
+
+    lax.fori_loop(0, count, to_spectrum, 0)
+
+    ids = lax.broadcasted_iota(jnp.int32, (table_ref.shape[1] // 3, wide), 0)
+
+    def hats(shell, frac):
+        return jnp.where(ids == shell, 1.0 - frac, jnp.where(ids == shell + 1, frac, 0.0))
+
+    def mix_rows(row_sets, load):
+        sums = [jnp.zeros((padded, wide), jnp.float32) for _ in range(2 * len(row_sets))]
+        for node in range(count):
+            part = phi[node * padded : (node + 1) * padded, :]
+            for at, row in enumerate(row_sets):
+                for e in range(2):
+                    sums[2 * at + e] = sums[2 * at + e] + part * load(node, e, row)
+        return sums
+
+    def step(i, carry):
+        weights = hats(shell_ref[pl.ds(i, 1), :], frac_ref[pl.ds(i, 1), :])
+        phi[...] = matmul(table_ref[...], triple_right(weights))
+        rows = [i, lax.rem(length - i, length)]
+        sums = mix_rows(rows, lambda node, e, row: spec[node, pl.ds(e * length + row, 1), :])
+        for at, row in enumerate(rows):
+            for e in range(2):
+                start = pl.multiple_of((e * length + row) * padded, SUBLANES)
+                for k in range(per):
+                    value = sums[2 * at + e][:, k * length : (k + 1) * length]
+                    mixed[k, pl.ds(start, padded), :] = value
+        return carry
+
+    lax.fori_loop(0, half + 1, step, 0)
+
+    extra[...] = jnp.zeros_like(extra)
+
+    @pl.when(joint)
+    def _():
+        right = jnp.concatenate(
+            [tx_ref[:, length : 2 * length], tx_ref[:, 3 * length : 4 * length]], axis=1
+        )
+
+        def gather(node, carry):
+            high, low = halves(block_of(node, 1))
+            imag = (matmul_nt(chosen, high) + matmul_nt(chosen, low))[:SUBLANES]
+            high, low = halves(-2.0 * imag)
+            zero = jnp.zeros_like(low)
+            left = jnp.concatenate(
+                [jnp.concatenate([high, high], 1), jnp.concatenate([low, zero], 1)], axis=0
+            )
+            delta = matmul_nt(left, right)
+            delta = delta[:SUBLANES] + delta[SUBLANES:]
+            spec[node, 0:SUBLANES, :] = delta
+            return carry
+
+        lax.fori_loop(0, count, gather, 0)
+        weights = 0.5 * (
+            hats(pair_shell_ref[0:1, :], pair_frac_ref[0:1, :])
+            - hats(pair_shell_ref[1:2, :], pair_frac_ref[1:2, :])
+        )
+        phi[...] = matmul(table_ref[...], triple_right(weights))
+
+        def load(node, e, row):
+            return jnp.concatenate(
+                [spec[node, r : r + 1, e * length : (e + 1) * length] for r in range(2)], axis=1
+            )
+
+        real, imag = mix_rows([0], load)
+        for r in range(2):
+            left = jnp.concatenate(
+                [real[:, r * length : (r + 1) * length], imag[:, r * length : (r + 1) * length]],
+                axis=1,
+            )
+            added = matmul_nt(triple_left(left), right_triple(ti_ref))
+            for c in range(2):
+                value = added[:, c * length : (c + 1) * length]
+                extra[c, pl.ds(r, padded, stride=SUBLANES), :] = value
+
+    def to_slabs(node, carry):
+        rows = [mixed[k, pl.ds(node, 2 * length, stride=padded), :] for k in range(per)]
+        out = matmul(ti_ref[...], triple_right(jnp.concatenate(rows, axis=1)))
+        place = pl.ds(pl.multiple_of(node * SUBLANES, SUBLANES), SUBLANES)
+        high, low = halves(jnp.concatenate([extra[c, place, :] for c in range(2)], axis=1))
+        both = jnp.concatenate([high, low], axis=0)
+        mask = jnp.concatenate([chosen[:SUBLANES], chosen[:SUBLANES]], axis=0)
+        out = out + matmul_tn(both, mask)
+        for c in range(2):
+            for k in range(per):
+                value = out[c * length : (c + 1) * length, k * length : (k + 1) * length]
+                send[:, k, c, node] = value.reshape(grid_size, grid_part, length)
+        return carry
+
+    def copy_of(at, j):
+        nodes = pl.ds(at * group, group)
+        return pltpu.make_async_remote_copy(
+            src_ref=send.at[order[j], :, :, nodes],
+            dst_ref=out_ref.at[me, :, :, nodes],
+            send_sem=sems.at[0, at, j],
+            recv_sem=sems.at[1, at, j],
+            device_id={"grid": order[j]},
+            device_id_type=MESH,
+        )
+
+    groups = count // group
+    for at in range(groups):
+        lax.fori_loop(at * group, (at + 1) * group, to_slabs, 0)
+        for j in range(grid_size - 1):
+            copy_of(at, j).start()
+    own = pltpu.make_async_copy(send.at[me], out_ref.at[me], sems.at[0, groups, 0])
+    own.start()
+    own.wait()
+    for at in range(groups):
+        for j in range(grid_size - 1):
+            copy_of(at, j).wait()
+
+
+def right_triple(ti_ref):
+    wide = ti_ref.shape[1] // 3
+    high, low = ti_ref[:, 0:wide], ti_ref[:, wide : 2 * wide]
+    return jnp.concatenate([high, high, low], axis=1)
+
+
+def middle(waves, shell, frac, pair_shell, pair_frac, kernel_table, tables, planes, grid_size):
+    count = kernel_table.shape[0]
+    length = waves.shape[-1]
+    per = planes // grid_size
+    padded = -(-count // SUBLANES) * SUBLANES
+    depth = -(-(kernel_table.shape[2]) // LANES) * LANES
+    table = jnp.pad(kernel_table, ((0, 0), (0, padded - count), (0, depth - kernel_table.shape[2])))
+    table = table.reshape(count * padded, depth)
+    rounded = lax.reduce_precision(table, exponent_bits=8, mantissa_bits=7)
+    high, low = rounded.astype(jnp.bfloat16), (table - rounded).astype(jnp.bfloat16)
+    table = jnp.concatenate([high, low, high], axis=1)
+    group = count // 4 if count % 4 == 0 else count
+    sizes = (count, padded, grid_size, planes, length, group)
+    grid_part = length // grid_size
+    wide = per * length
+    shape = (grid_size, per, 2, count, grid_part, length)
+    return pl.pallas_call(
+        lambda *refs: middle_kernel(sizes, *refs),
+        in_specs=[pl.BlockSpec(memory_space=VMEM)] * 8,
+        out_specs=pl.BlockSpec(memory_space=VMEM),
+        out_shape=jax.ShapeDtypeStruct(shape, jnp.float32),
+        scratch_shapes=[
+            VMEM((count, 2 * length, wide), jnp.float32),
+            VMEM((per, 2 * length * padded, length), jnp.float32),
+            VMEM((count * padded, wide), jnp.float32),
+            VMEM((2, padded * SUBLANES, length), jnp.float32),
+            VMEM(shape, jnp.float32),
+            pltpu.SemaphoreType.DMA((2, count // group + 1, grid_size - 1)),
+        ],
+        compiler_params=pltpu.CompilerParams(
+            collective_id=2, has_side_effects=True, vmem_limit_bytes=60 * 2**20
+        ),
+    )(waves, shell, frac, pair_shell, pair_frac, table, tables["x_forward"], tables["x_backward"])
+
+
+def last_kernel(sizes, back_ref, index_ref, slope_ref, tz_ref, ty_ref, out_ref, slab, turned, ids):
+    count, planes, grid_part, length = sizes
+    band_at = lax.axis_index("band")
+    rows = count * grid_part
+
+    def to_rows(plane, carry):
+        kind = jnp.minimum(plane + band_at * planes, 1)
+        parts = 4
+        size = rows // parts
+        for at in range(parts):
+            left = jnp.concatenate(
+                [back_ref[plane, c, at * size : (at + 1) * size, :] for c in range(2)], axis=1
+            )
+            out = matmul(triple_left(left), ty_ref[kind])
+            for c in range(2):
+                start = pl.multiple_of((c * planes + plane) * rows + at * size, SUBLANES)
+                slab[pl.ds(start, size), :] = out[:, c * length : (c + 1) * length]
+        return carry
+
+    lax.fori_loop(0, planes, to_rows, 0)
+    table = tz_ref[band_at]
+
+    def pair_of(pair, carry):
+        for side in range(2):
+            x_at = pair * 2 + side
+            lanes = slice(side * length, (side + 1) * length)
+            ids[:, lanes] = index_ref[x_at].T - 1
+            for j in range(4):
+                turned[j, :, lanes] = slope_ref[j, x_at].T
+
+        def add_node(node, total):
+            start = node * grid_part + pair * 2
+            sides = []
+            for side in range(2):
+                parts = [
+                    slab[pl.ds(c * planes * rows + start + side, planes, stride=rows), :]
+                    for c in range(2)
+                ]
+                sides.append(jnp.concatenate(parts, axis=0))
+            field = matmul(table, triple_right(jnp.concatenate(sides, axis=1)))
+            index = ids[...]
+            slope = jnp.where(index == node, turned[0], 0.0)
+            for j in range(1, 4):
+                slope = jnp.where(index == node - j, turned[j], slope)
+            return total + field * slope
+
+        total = lax.fori_loop(0, count, add_node, jnp.zeros((length, 2 * length), jnp.float32))
+        for side in range(2):
+            out_ref[pair * 2 + side] = total[:, side * length : (side + 1) * length].T
+        return carry
+
+    lax.fori_loop(0, grid_part // 2, pair_of, 0)
+
+
+def last(returned, node_index, node_slope, tables, count, planes):
+    grid_part, length = node_index.shape[:2]
+    sizes = (count, planes, grid_part, length)
+    rows = count * grid_part
+    returned = returned.reshape(planes, 2, rows, length)
+    return pl.pallas_call(
+        lambda *refs: last_kernel(sizes, *refs),
+        in_specs=[pl.BlockSpec(memory_space=VMEM)] * 5,
+        out_specs=pl.BlockSpec(memory_space=VMEM),
+        out_shape=jax.ShapeDtypeStruct(node_index.shape, jnp.float32),
+        scratch_shapes=[
+            VMEM((2 * planes * rows, length), jnp.float32),
+            VMEM((4, length, 2 * length), jnp.float32),
+            VMEM((length, 2 * length), jnp.int32),
+        ],
+        compiler_params=pltpu.CompilerParams(vmem_limit_bytes=60 * 2**20),
+    )(returned, node_index, node_slope, tables["z_backward"], tables["y_backward"])
+
+
+def fused_per_device(tables, partial_density, node_index, node_weight, node_slope, kernel_table):
+    length = node_index.shape[1]
+    half = length // 2
+    count = kernel_table.shape[0]
+    planes = half // lax.axis_size("band")
+    grid_size = lax.axis_size("grid")
+    per = planes // grid_size
+    band_at, grid_at = lax.axis_index("band"), lax.axis_index("grid")
+    density = band_sum(partial_density[0], 0)
+    waves = forward(density, node_index, node_weight, tables, count, planes, grid_size)
+
+    full_range = jnp.arange(length, dtype=jnp.int32)
+    own_planes = band_at * planes + grid_at * per + jnp.arange(per, dtype=jnp.int32)
+    freq = frequency_of(full_range, length)
+    third = jnp.where(
+        (own_planes[:, None] == 0) & (full_range[None] > half),
+        half * half,
+        (own_planes * own_planes)[:, None],
+    )
+    base = (third + (freq * freq)[None]).reshape(per * length)
+    steps = jnp.arange(half + 1, dtype=jnp.int32)
+    shell, frac = shell_split(base[None] + (steps * steps)[:, None])
+    pair = jnp.concatenate([freq * freq, freq * freq + half * half])
+    pair = jnp.pad(pair, (0, per * length - 2 * length))
+    pair_shell, pair_frac = shell_split(jnp.stack([pair, pair + half * half]))
+    returned = middle(
+        waves, shell, frac, pair_shell, pair_frac, kernel_table, tables, planes, grid_size
+    )
+    potential = last(returned, node_index, node_slope, tables, count, planes)
+    return band_sum(potential, 3)
+
+
+def fits(mesh, length, groups):
+    bands, grids = mesh.shape["band"], mesh.shape["grid"]
+    planes = length // 2 // bands
+    return (
+        length == LANES
+        and planes == SUBLANES
+        and planes % grids == 0
+        and planes // grids >= 2
+        and bands % 2 == 0
+        and (length // grids) % max(SUBLANES, bands) == 0
+    )
+
+
 def solution(mesh):
     placed = (
         P("band", "grid", None, None),
@@ -228,6 +861,17 @@
         P(None, "grid", None, None),
         P(),
     )
-    return jax.shard_map(
-        per_device, mesh=mesh, in_specs=placed, out_specs=P("grid", None, None), check_vma=False
-    )
+
+    def program(*args):
+        length = args[1].shape[0]
+        body = per_device
+        if fits(mesh, length, args[0].shape[0]):
+            bands = mesh.shape["band"]
+            tables = constant_tables(length, bands, length // 2 // bands)
+            tables = {name: jnp.asarray(table) for name, table in tables.items()}
+            body = lambda *blocks: fused_per_device(tables, *blocks)
+        return jax.shard_map(
+            body, mesh=mesh, in_specs=placed, out_specs=P("grid", None, None), check_vma=False
+        )(*args)
+
+    return program

time: 761 us -> 392 us (0.52)
  Pallas kernels: 40.6 us -> 379 us
  waiting for transfers between devices: 306 us -> 0 us
  matrix products: 161 us -> 0 us
  local copies, waits for them, and re-layouts: 158 us -> 4.1 us
  other arithmetic: 46.6 us -> 3.06 us
  starting transfers between devices: 23.1 us -> 0 us
  between operations: 14 us -> 0.08 us
    pallas_call x1 -> x5, Pallas kernels: 40.6 us -> 379 us  [the longest x2 141 us: band_sum(): pl.pallas_call(lambda *refs: sum_kernel(outer, *refs), in_specs=[pl.Block...]
    psum x2 -> x0, waiting for transfers between devices: 200 us -> none  [the longest x1 101 us: per_device(): return lax.psum(partial_potential, 'band')]
    dot_general x7 -> x0, matrix products: 161 us -> none  [the longest x6 161 us: short(): return jnp.einsum(pattern, left, right, precision=lax.Precision.HIGH)]
    all_to_all x2 -> x0, waiting for transfers between devices: 105 us -> none  [the longest x1 54.2 us: per_device(): lax.all_to_all(waves, 'grid', split_axis=0, concat_axis=0, tiled=True)]
    unnamed x20 -> x1, local copies, waits for them, and re-layouts: 86.5 us -> 3.14 us
    reshape x2 -> x0, local copies, waits for them, and re-layouts: 39.4 us -> none  [per_device(): waves = waves.reshape((grid_size, grid_part) + waves.shape[1:])]
    all_to_all x2 -> x0, other arithmetic: 35.9 us -> none  [the longest x1 18 us: per_device(): lax.all_to_all(inverse, 'grid', split_axis=0, concat_axis=0, tiled=True)]
    all_to_all x2 -> x0, starting transfers between devices: 23.1 us -> none  [the longest x1 17 us: per_device(): lax.all_to_all(waves, 'grid', split_axis=0, concat_axis=0, tiled=True)]
  transfers between devices with their start and end apart: 4 -> 0, of which waited for: 4 -> 0; matrix products, arithmetic and copies ran while one was open for 3% -> 0% of each run, Pallas kernels for 0% -> 0%
where the time goes in v1:
time: 392 us; the launch traced here: 386 us
  Pallas kernels  379 us (97%)
  local copies, waits for them, and re-layouts  4.1 us (1%)
    pallas_call x2, Pallas kernels, band_sum(): pl.pallas_call(lambda *refs: sum_kernel(outer, *refs), in_specs=[pl.Block...  141 us
    pallas_call x1, Pallas kernels, middle(): pl.pallas_call(lambda *refs: middle_kernel(sizes, *refs), in_specs=[pl.Bl...  92.5 us
    pallas_call x1, Pallas kernels, forward(): pl.pallas_call(lambda *refs: forward_kernel(sizes, *refs), in_specs=[pl.B...  76.7 us
    pallas_call x1, Pallas kernels, last(): pl.pallas_call(lambda *refs: last_kernel(sizes, *refs), in_specs=[pl.Bloc...  69.5 us

profile of v1, /device:TPU:1, one launch (start us, length us, event | category | flops | bytes accessed | tf_op | source)
XLA Modules:
  0.0 386.4 jit_solution(7890247991409906031)
XLA Ops:
  0.1 0.1 fusion.9
  0.2 0.6 convert_subtract_fusion
  0.8 0.8 convert_add_fusion.refs_1_
  1.5 0.8 fusion.2.refs_2_
  2.3 1.0 pad.4
  3.3 0.8 pad_maximum_fusion.refs_5_
  4.1 68.1 %shard_map.109.refs_0_ = f32[32,128,128]{2,1,0:T(8,128)} custom-call(f32[32,128,128]{2,1,0:T(8,128)} %bitcast.13), custom_call_target="tpu_custom_call" | custom-call | tf_op jit(solution)/shard_map/pallas_call | solution.py:404
  72.2 76.7 %shard_map.110.refs_0_ = f32[2,2,16,160,128]{4,3,2,1,0:T(8,128)} custom-call(f32[32,128,128]{2,1,0:T(8,128)} %shard_map.109.refs_0_, s32[32,128,128]{2,1,0:T(8,128)} %refs_1_.3, f32[4,32,128,128]{3,2,1,0:T(8,128)} %refs_2_.2, bf16[8,32,256]{2,1,0:T(8,128)(2,1)} %constant.43.clone.refs_3_, bf16[2,768,256]{2,1,0:T(8,128)(2,1)} %constant.44.clone.refs_4_), custom_call_target="tpu_custom_call" | custom-call | tf_op jit(solution)/shard_map/pallas_call | solution.py:520
  148.9 92.5 %shard_map.111 = f32[4,2,2,20,32,128]{5,4,3,2,1,0:T(8,128)} custom-call(f32[2,2,16,160,128]{4,3,2,1,0:T(8,128)} %shard_map.110.refs_0_, s32[65,256]{1,0:T(8,128)} %convert_add_fusion.refs_1_, f32[65,256]{1,0:T(8,128)} %fusion.2.refs_2_, s32[2,256]{1,0:T(2,128)} %get-tuple-element.6.refs_3_, f32[2,256]{1,0:T(2,128)} %get-tuple-element.5.refs_4_, ...), custom_call_target="tpu_custom_call" | custom-call | tf_op jit(solution)/shard_map/pallas_call | solution.py:719
  241.4 69.5 %shard_map.112.refs_0_ = f32[32,128,128]{2,1,0:T(8,128)} custom-call(f32[8,2,640,128]{3,2,1,0:T(8,128)} %bitcast.12, s32[32,128,128]{2,1,0:T(8,128)} %refs_1_.3, f32[4,32,128,128]{3,2,1,0:T(8,128)} %refs_2_.3, bf16[8,128,48]{2,1,0:T(8,128)(2,1)} %constant.47.clone.refs_3_, bf16[2,768,256]{2,1,0:T(8,128)(2,1)} %constant.48.clone.refs_4_), custom_call_target="tpu_custom_call" | custom-call | tf_op jit(solution)/shard_map/pallas_call | solution.py:797
  310.9 72.4 %shard_map.113 = f32[32,128,128]{2,1,0:T(8,128)} custom-call(f32[32,128,128]{2,1,0:T(8,128)} %shard_map.112.refs_0_), custom_call_target="tpu_custom_call" | custom-call | tf_op jit(solution)/shard_map/pallas_call | solution.py:404
  383.3 3.1 copy.13
  (9 shorter events, 0.1 us)

commit v2 on v1

--- a/solution.py
+++ b/solution.py
@@ -327,107 +327,143 @@
     )
 
 
-def greet(axis, targets):
+def greet(targets):
     barrier = pltpu.get_barrier_semaphore()
-    for target in targets:
+    for axis, target in targets:
         pl.semaphore_signal(barrier, inc=1, device_id={axis: target}, device_id_type=MESH)
     pl.semaphore_wait(barrier, len(targets))
 
 
-def sum_kernel(outer, in_ref, out_ref, near_buf, stage, far_buf, sems):
-    me = lax.axis_index("band")
-    far, near = me // 2, lax.rem(me, 2)
-    partner = far * 2 + (1 - near)
-    others = [lax.rem(far + 1 + j, outer) for j in range(outer)]
-    back = [lax.rem(far + outer - 1 - j, outer) for j in range(outer)]
-    rows = in_ref.shape[0] // 2
-    part = rows // outer
-    greet("band", [partner] + [o * 2 + near for o in others[:-1]])
-
-    def piece(side, quarter):
-        return pl.ds(side * rows + quarter * part, part)
-
-    def remote(src, dst, row, j, target):
+class BandSum:
+    def __init__(self, outer, chunk_rows, src, dst, near_buf, stage, far_buf, sems):
+        me = lax.axis_index("band")
+        self.outer, self.src, self.dst = outer, src, dst
+        self.near_buf, self.stage, self.far_buf, self.sems = near_buf, stage, far_buf, sems
+        self.far, self.near = me // 2, lax.rem(me, 2)
+        self.partner = self.far * 2 + (1 - self.near)
+        self.others = [lax.rem(self.far + 1 + j, outer) for j in range(outer)]
+        self.back = [lax.rem(self.far + outer - 1 - j, outer) for j in range(outer)]
+        self.chunk_rows = chunk_rows
+        self.side_rows = chunk_rows // 2
+        self.part = self.side_rows // outer
+        self.peers = [("band", self.partner)] + [
+            ("band", o * 2 + self.near) for o in self.others[:-1]
+        ]
+
+    def piece(self, chunk, side, quarter):
+        start = chunk * self.chunk_rows + side * self.side_rows + quarter * self.part
+        return pl.ds(start, self.part)
+
+    def copy(self, src, dst, chunk, kind, j, target):
         return pltpu.make_async_remote_copy(
             src_ref=src,
             dst_ref=dst,
-            send_sem=sems.at[row, 0, j],
-            recv_sem=sems.at[row, 1, j],
+            send_sem=self.sems.at[chunk, kind, 0, j],
+            recv_sem=self.sems.at[chunk, kind, 1, j],
             device_id={"band": target},
             device_id_type=MESH,
         )
 
-    near_copies = [
-        remote(in_ref.at[piece(1 - near, others[j])], near_buf.at[j], 0, j, partner)
-        for j in range(outer)
+    def near_copy(self, c, j):
+        src = self.src.at[self.piece(c, 1 - self.near, self.others[j])]
+        return self.copy(src, self.near_buf.at[c, j], c, 0, j, self.partner)
+
+    def far_copy(self, c, j):
+        target = self.others[j] * 2 + self.near
+        return self.copy(self.stage.at[c, j], self.far_buf.at[c, j], c, 1, j, target)
+
+    def gather_copy(self, c, j):
+        own = self.dst.at[self.piece(c, self.near, self.far)]
+        return self.copy(own, own, c, 2, j, self.others[j] * 2 + self.near)
+
+    def pass_copy(self, c, j):
+        block = self.dst.at[self.piece(c, self.near, self.back[j])]
+        return self.copy(block, block, c, 3, j, self.partner)
+
+    def start(self, c):
+        for j in range(self.outer):
+            self.near_copy(c, j).start()
+
+    def reduce(self, c):
+        for j in range(self.outer - 1):
+            self.near_copy(c, j).wait_recv()
+            mine = self.src[self.piece(c, self.near, self.others[j])]
+            self.stage[c, j] = mine + self.near_buf[c, j]
+            self.far_copy(c, j).start()
+
+    def finish(self, c):
+        last = self.outer - 1
+        self.near_copy(c, last).wait_recv()
+        own = self.piece(c, self.near, self.far)
+        total = self.src[own] + self.near_buf[c, last]
+        for j in range(last):
+            self.far_copy(c, j).wait_recv()
+            total = total + self.far_buf[c, j]
+        self.dst[own] = total
+        for j in range(last):
+            self.gather_copy(c, j).start()
+        self.pass_copy(c, last).start()
+
+    def forward(self, c):
+        for j in range(self.outer - 1):
+            self.gather_copy(c, j).wait_recv()
+            self.pass_copy(c, j).start()
+
+    def arrive(self, c):
+        for j in range(self.outer):
+            self.pass_copy(c, j).wait_recv()
+
+    def drain(self, c):
+        for j in range(self.outer):
+            self.near_copy(c, j).wait_send()
+            self.pass_copy(c, j).wait_send()
+        for j in range(self.outer - 1):
+            self.far_copy(c, j).wait_send()
+            self.gather_copy(c, j).wait_send()
+
+
+def band_scratch(outer, chunks, shape):
+    part = (shape[0] // chunks // (2 * outer),) + shape[1:]
+    return [
+        VMEM((chunks, outer) + part, jnp.float32),
+        VMEM((chunks, outer - 1) + part, jnp.float32),
+        VMEM((chunks, outer - 1) + part, jnp.float32),
+        pltpu.SemaphoreType.DMA((chunks, 4, 2, outer)),
     ]
-    for copy in near_copies:
-        copy.start()
-    far_copies = []
-    for j in range(outer - 1):
-        near_copies[j].wait_recv()
-        stage[j] = in_ref[piece(near, others[j])] + near_buf[j]
-        copy = remote(stage.at[j], far_buf.at[j], 1, j, others[j] * 2 + near)
-        copy.start()
-        far_copies.append(copy)
-    near_copies[outer - 1].wait_recv()
-    total = in_ref[piece(near, far)] + near_buf[outer - 1]
-    for copy in far_copies:
-        copy.wait_recv()
-    for j in range(outer - 1):
-        total = total + far_buf[j]
-    own = piece(near, far)
-    out_ref[own] = total
-    gathers = []
-    for j in range(outer - 1):
-        copy = remote(out_ref.at[own], out_ref.at[own], 2, j, others[j] * 2 + near)
-        copy.start()
-        gathers.append(copy)
-    passes = [remote(out_ref.at[own], out_ref.at[own], 3, outer - 1, partner)]
-    passes[0].start()
-    for j in range(outer - 1):
-        gathers[j].wait_recv()
-        block = out_ref.at[piece(near, back[j])]
-        copy = remote(block, block, 3, j, partner)
-        copy.start()
-        passes.append(copy)
-    for copy in passes:
-        copy.wait_recv()
-    for copy in near_copies + far_copies + gathers + passes:
-        copy.wait_send()
-
-
-def band_sum(values, collective_id):
-    outer = lax.axis_size("band") // 2
-    part = values.shape[0] // (2 * outer)
-    piece = (part,) + values.shape[1:]
-    return pl.pallas_call(
-        lambda *refs: sum_kernel(outer, *refs),
-        in_specs=[pl.BlockSpec(memory_space=VMEM)],
-        out_specs=pl.BlockSpec(memory_space=VMEM),
-        out_shape=jax.ShapeDtypeStruct(values.shape, jnp.float32),
-        scratch_shapes=[
-            VMEM((outer,) + piece, jnp.float32),
-            VMEM((outer - 1,) + piece, jnp.float32),
-            VMEM((outer - 1,) + piece, jnp.float32),
-            pltpu.SemaphoreType.DMA((4, 2, outer)),
-        ],
-        compiler_params=pltpu.CompilerParams(
-            collective_id=collective_id, has_side_effects=True, vmem_limit_bytes=60 * 2**20
-        ),
-    )(values)
 
 
 def forward_kernel(
-    sizes, density_ref, index_ref, weight_ref, tz_ref, ty_ref, out_ref, theta, columns, send, sems
+    sizes,
+    partial_ref,
+    index_hbm,
+    weight_hbm,
+    tz_ref,
+    ty_ref,
+    out_ref,
+    density_ref,
+    index_ref,
+    weight_ref,
+    theta,
+    columns,
+    send,
+    sems,
+    load_sems,
+    *band_refs,
 ):
-    count, grid_size, steps, planes, length = sizes
+    count, grid_size, steps, planes, length, outer = sizes
+    index_load = pltpu.make_async_copy(index_hbm, index_ref, load_sems.at[0])
+    weight_load = pltpu.make_async_copy(weight_hbm, weight_ref, load_sems.at[1])
+    band = BandSum(outer, SUBLANES, partial_ref, density_ref, *band_refs)
     step_rows = SUBLANES * length
     band_at, me = lax.axis_index("band"), lax.axis_index("grid")
     order = [lax.rem(me + 1 + j, grid_size) for j in range(grid_size)]
     per = planes // grid_size
     rows = count * SUBLANES
-    greet("grid", order[:-1])
+    greet(band.peers + [("grid", target) for target in order[:-1]])
+    for step in range(steps):
+        band.start(step)
+    index_load.start()
+    weight_load.start()
 
     def copy_of(step, slot, j):
         return pltpu.make_async_remote_copy(
@@ -494,46 +530,73 @@
                 else:
                     out_ref[k, d, me * steps + step] = value
 
+    todo = []
+    for at in range(steps + 3):
+        for call, lag in ((band.reduce, 0), (band.finish, 1), (band.forward, 2)):
+            if 0 <= at - lag < steps:
+                todo.append((call, at - lag))
+    ahead = todo.index((band.forward, 0)) + 1
+
+    def advance(number):
+        for call, chunk in todo[:number]:
+            call(chunk)
+        del todo[:number]
+
+    advance(ahead)
+    index_load.wait()
+    weight_load.wait()
     for step in range(steps):
         slot = step % 2
+        band.arrive(step)
         fill(step)
+        advance(1)
         columns_of(step)
         for j in range(grid_size):
+            advance(1 if step == 0 else len(todo))
             if step >= 2 and j < grid_size - 1:
                 copy_of(step - 2, slot, j).wait_send()
             waves_of(step, slot, j)
             if j < grid_size - 1:
                 copy_of(step, slot, j).start()
     for step in range(steps):
+        band.drain(step)
         for j in range(grid_size - 1):
             if step >= steps - 2:
                 copy_of(step, step % 2, j).wait_send()
             copy_of(step, step % 2, j).wait_recv()
 
 
-def forward(density, node_index, node_weight, tables, count, planes, grid_size):
-    grid_part, length = density.shape[:2]
+def forward(partial, node_index, node_weight, tables, count, planes, grid_size):
+    grid_part, length = partial.shape[:2]
+    outer = lax.axis_size("band") // 2
     steps = grid_part // SUBLANES
     per = planes // grid_size
-    sizes = (count, grid_size, steps, planes, length)
+    sizes = (count, grid_size, steps, planes, length, outer)
     rows = count * SUBLANES
+    whole = pl.BlockSpec(memory_space=VMEM)
+    anywhere = pl.BlockSpec(memory_space=pl.ANY)
     return pl.pallas_call(
         lambda *refs: forward_kernel(sizes, *refs),
-        in_specs=[pl.BlockSpec(memory_space=VMEM)] * 5,
-        out_specs=pl.BlockSpec(memory_space=VMEM),
+        in_specs=[whole, anywhere, anywhere, whole, whole],
+        out_specs=whole,
         out_shape=jax.ShapeDtypeStruct(
             (per, 2, grid_size * steps, rows, length), jnp.float32
         ),
         scratch_shapes=[
+            VMEM(partial.shape, jnp.float32),
+            VMEM(node_index.shape, jnp.int32),
+            VMEM(node_weight.shape, jnp.float32),
             VMEM((count, SUBLANES * length, 2 * length), jnp.bfloat16),
             VMEM((2 * planes * rows, length), jnp.float32),
             VMEM((2, grid_size - 1, per, 2, rows, length), jnp.float32),
             pltpu.SemaphoreType.DMA((2, steps, grid_size - 1)),
-        ],
+            pltpu.SemaphoreType.DMA((2,)),
+        ]
+        + band_scratch(outer, steps, partial.shape),
         compiler_params=pltpu.CompilerParams(
             collective_id=1, has_side_effects=True, vmem_limit_bytes=60 * 2**20
         ),
-    )(density, node_index, node_weight, tables["z_forward"], tables["y_forward"])
+    )(partial, node_index, node_weight, tables["z_forward"], tables["y_forward"])
 
 
 def middle_kernel(
@@ -546,23 +609,45 @@
     table_ref,
     tx_ref,
     ti_ref,
+    index_hbm,
+    slope_hbm,
+    tz_ref,
+    ty_ref,
     out_ref,
     spec,
     mixed,
     phi,
     extra,
     send,
+    back,
+    index_ref,
+    slope_ref,
+    slab,
+    turned,
+    ids_ref,
+    fields,
+    total_ref,
+    potential,
     sems,
+    load_sems,
+    *band_refs,
 ):
-    count, padded, grid_size, planes, length, group = sizes
+    count, padded, grid_size, planes, length, outer = sizes
+    index_load = pltpu.make_async_copy(index_hbm, index_ref, load_sems.at[0])
+    slope_load = pltpu.make_async_copy(slope_hbm, slope_ref, load_sems.at[1])
+    index_load.start()
+    slope_load.start()
+    band = BandSum(outer, SUBLANES, potential, out_ref, *band_refs)
     per = planes // grid_size
     grid_part = length // grid_size
     wide = per * length
     half = length // 2
     band_at, me = lax.axis_index("band"), lax.axis_index("grid")
     order = [lax.rem(me + 1 + j, grid_size) for j in range(grid_size)]
+    steps = grid_part // SUBLANES
+    rows = count * SUBLANES
     joint = (band_at == 0) & (me == 0)
-    greet("grid", order[:-1])
+    greet(band.peers + [("grid", target) for target in order[:-1]])
 
     lane = lax.broadcasted_iota(jnp.int32, (16, wide), 1)
     slot = lax.broadcasted_iota(jnp.int32, (16, wide), 0)
@@ -667,31 +752,108 @@
         for c in range(2):
             for k in range(per):
                 value = out[c * length : (c + 1) * length, k * length : (k + 1) * length]
-                send[:, k, c, node] = value.reshape(grid_size, grid_part, length)
+                value = value.reshape(grid_size, steps, SUBLANES, length)
+                place = pl.ds(pl.multiple_of(node * SUBLANES, SUBLANES), SUBLANES)
+                send[:, :, k, c, place, :] = value
         return carry
 
-    def copy_of(at, j):
-        nodes = pl.ds(at * group, group)
+    def copy_of(step, j):
         return pltpu.make_async_remote_copy(
-            src_ref=send.at[order[j], :, :, nodes],
-            dst_ref=out_ref.at[me, :, :, nodes],
-            send_sem=sems.at[0, at, j],
-            recv_sem=sems.at[1, at, j],
+            src_ref=send.at[order[j], step],
+            dst_ref=back.at[step, me],
+            send_sem=sems.at[0, step, j],
+            recv_sem=sems.at[1, step, j],
             device_id={"grid": order[j]},
             device_id_type=MESH,
         )
 
-    groups = count // group
-    for at in range(groups):
-        lax.fori_loop(at * group, (at + 1) * group, to_slabs, 0)
+    def own_copy(step):
+        return pltpu.make_async_copy(
+            send.at[me, step], back.at[step, me], sems.at[0, step, grid_size - 1]
+        )
+
+    lax.fori_loop(0, count, to_slabs, 0)
+    for step in range(steps):
         for j in range(grid_size - 1):
-            copy_of(at, j).start()
-    own = pltpu.make_async_copy(send.at[me], out_ref.at[me], sems.at[0, groups, 0])
-    own.start()
-    own.wait()
-    for at in range(groups):
+            copy_of(step, j).start()
+        own_copy(step).start()
+    index_load.wait()
+    slope_load.wait()
+    table = tz_ref[band_at]
+
+    def y_rows(step):
+        def body(plane, carry):
+            kind = jnp.minimum(plane + band_at * planes, 1)
+            left = jnp.concatenate(
+                [back[step, plane // per, lax.rem(plane, per), c] for c in range(2)], axis=1
+            )
+            out = matmul(triple_left(left), ty_ref[kind])
+            for c in range(2):
+                start = pl.multiple_of((c * planes + plane) * rows, SUBLANES)
+                slab[pl.ds(start, rows), :] = out[:, c * length : (c + 1) * length]
+            return carry
+
+        lax.fori_loop(0, planes, body, 0)
+
+    def z_rows(step):
+        def pair_of(pair, carry):
+            first = step * SUBLANES + pair * 2
+            for side in range(2):
+                lanes = slice(side * length, (side + 1) * length)
+                ids_ref[:, lanes] = index_ref[first + side].T - 1
+                for j in range(4):
+                    turned[j, :, lanes] = slope_ref[j, first + side].T
+            for node in range(count):
+                sides = []
+                for side in range(2):
+                    start = node * SUBLANES + pair * 2 + side
+                    parts = [
+                        slab[pl.ds(c * planes * rows + start, planes, stride=rows), :]
+                        for c in range(2)
+                    ]
+                    sides.append(jnp.concatenate(parts, axis=0))
+                fields[node] = matmul(table, triple_right(jnp.concatenate(sides, axis=1)))
+
+            def pick(block, carry):
+                place = pl.ds(pl.multiple_of(block * SUBLANES, SUBLANES), SUBLANES)
+                index = ids_ref[place, :]
+                picked = [jnp.zeros((SUBLANES, 2 * length), jnp.float32) for _ in range(4)]
+                for node in range(count):
+                    field = fields[node, place, :]
+                    for j in range(4):
+                        picked[j] = jnp.where(index == node - j, field, picked[j])
+                summed = picked[0] * turned[0, place, :]
+                for j in range(1, 4):
+                    summed = summed + picked[j] * turned[j, place, :]
+                total_ref[place, :] = summed
+                return carry
+
+            lax.fori_loop(0, length // SUBLANES, pick, 0)
+            for side in range(2):
+                lanes = slice(side * length, (side + 1) * length)
+                potential[first + side] = total_ref[:, lanes].T
+            return carry
+
+        lax.fori_loop(0, SUBLANES // 2, pair_of, 0)
+
+    calls = ((band.forward, 3), (band.finish, 2), (band.reduce, 1))
+    for at in range(steps + 3):
+        if at < steps:
+            own_copy(at).wait()
+            for j in range(grid_size - 1):
+                copy_of(at, j).wait_recv()
+            y_rows(at)
+        for call, lag in calls:
+            if 0 <= at - lag < steps:
+                call(at - lag)
+        if at < steps:
+            z_rows(at)
+            band.start(at)
+    for step in range(steps):
+        band.arrive(step)
+        band.drain(step)
         for j in range(grid_size - 1):
-            copy_of(at, j).wait()
+            copy_of(step, j).wait_send()
 
 
 def right_triple(ti_ref):
@@ -700,9 +862,12 @@
     return jnp.concatenate([high, high, low], axis=1)
 
 
-def middle(waves, shell, frac, pair_shell, pair_frac, kernel_table, tables, planes, grid_size):
+def backward(
+    waves, shells, node_index, node_slope, kernel_table, tables, planes, grid_size
+):
     count = kernel_table.shape[0]
     length = waves.shape[-1]
+    outer = lax.axis_size("band") // 2
     per = planes // grid_size
     padded = -(-count // SUBLANES) * SUBLANES
     depth = -(-(kernel_table.shape[2]) // LANES) * LANES
@@ -711,101 +876,51 @@
     rounded = lax.reduce_precision(table, exponent_bits=8, mantissa_bits=7)
     high, low = rounded.astype(jnp.bfloat16), (table - rounded).astype(jnp.bfloat16)
     table = jnp.concatenate([high, low, high], axis=1)
-    group = count // 4 if count % 4 == 0 else count
-    sizes = (count, padded, grid_size, planes, length, group)
+    sizes = (count, padded, grid_size, planes, length, outer)
     grid_part = length // grid_size
+    steps = grid_part // SUBLANES
     wide = per * length
-    shape = (grid_size, per, 2, count, grid_part, length)
+    rows = count * SUBLANES
+    whole = pl.BlockSpec(memory_space=VMEM)
+    anywhere = pl.BlockSpec(memory_space=pl.ANY)
     return pl.pallas_call(
         lambda *refs: middle_kernel(sizes, *refs),
-        in_specs=[pl.BlockSpec(memory_space=VMEM)] * 8,
-        out_specs=pl.BlockSpec(memory_space=VMEM),
-        out_shape=jax.ShapeDtypeStruct(shape, jnp.float32),
+        in_specs=[whole] * 8 + [anywhere] * 2 + [whole] * 2,
+        out_specs=whole,
+        out_shape=jax.ShapeDtypeStruct(node_index.shape, jnp.float32),
         scratch_shapes=[
             VMEM((count, 2 * length, wide), jnp.float32),
             VMEM((per, 2 * length * padded, length), jnp.float32),
             VMEM((count * padded, wide), jnp.float32),
             VMEM((2, padded * SUBLANES, length), jnp.float32),
-            VMEM(shape, jnp.float32),
-            pltpu.SemaphoreType.DMA((2, count // group + 1, grid_size - 1)),
-        ],
-        compiler_params=pltpu.CompilerParams(
-            collective_id=2, has_side_effects=True, vmem_limit_bytes=60 * 2**20
-        ),
-    )(waves, shell, frac, pair_shell, pair_frac, table, tables["x_forward"], tables["x_backward"])
-
-
-def last_kernel(sizes, back_ref, index_ref, slope_ref, tz_ref, ty_ref, out_ref, slab, turned, ids):
-    count, planes, grid_part, length = sizes
-    band_at = lax.axis_index("band")
-    rows = count * grid_part
-
-    def to_rows(plane, carry):
-        kind = jnp.minimum(plane + band_at * planes, 1)
-        parts = 4
-        size = rows // parts
-        for at in range(parts):
-            left = jnp.concatenate(
-                [back_ref[plane, c, at * size : (at + 1) * size, :] for c in range(2)], axis=1
-            )
-            out = matmul(triple_left(left), ty_ref[kind])
-            for c in range(2):
-                start = pl.multiple_of((c * planes + plane) * rows + at * size, SUBLANES)
-                slab[pl.ds(start, size), :] = out[:, c * length : (c + 1) * length]
-        return carry
-
-    lax.fori_loop(0, planes, to_rows, 0)
-    table = tz_ref[band_at]
-
-    def pair_of(pair, carry):
-        for side in range(2):
-            x_at = pair * 2 + side
-            lanes = slice(side * length, (side + 1) * length)
-            ids[:, lanes] = index_ref[x_at].T - 1
-            for j in range(4):
-                turned[j, :, lanes] = slope_ref[j, x_at].T
-
-        def add_node(node, total):
-            start = node * grid_part + pair * 2
-            sides = []
-            for side in range(2):
-                parts = [
-                    slab[pl.ds(c * planes * rows + start + side, planes, stride=rows), :]
-                    for c in range(2)
-                ]
-                sides.append(jnp.concatenate(parts, axis=0))
-            field = matmul(table, triple_right(jnp.concatenate(sides, axis=1)))
-            index = ids[...]
-            slope = jnp.where(index == node, turned[0], 0.0)
-            for j in range(1, 4):
-                slope = jnp.where(index == node - j, turned[j], slope)
-            return total + field * slope
-
-        total = lax.fori_loop(0, count, add_node, jnp.zeros((length, 2 * length), jnp.float32))
-        for side in range(2):
-            out_ref[pair * 2 + side] = total[:, side * length : (side + 1) * length].T
-        return carry
-
-    lax.fori_loop(0, grid_part // 2, pair_of, 0)
-
-
-def last(returned, node_index, node_slope, tables, count, planes):
-    grid_part, length = node_index.shape[:2]
-    sizes = (count, planes, grid_part, length)
-    rows = count * grid_part
-    returned = returned.reshape(planes, 2, rows, length)
-    return pl.pallas_call(
-        lambda *refs: last_kernel(sizes, *refs),
-        in_specs=[pl.BlockSpec(memory_space=VMEM)] * 5,
-        out_specs=pl.BlockSpec(memory_space=VMEM),
-        out_shape=jax.ShapeDtypeStruct(node_index.shape, jnp.float32),
-        scratch_shapes=[
+            VMEM((grid_size, steps, per, 2, rows, length), jnp.float32),
+            VMEM((steps, grid_size, per, 2, rows, length), jnp.float32),
+            VMEM(node_index.shape, jnp.int32),
+            VMEM(node_slope.shape, jnp.float32),
             VMEM((2 * planes * rows, length), jnp.float32),
             VMEM((4, length, 2 * length), jnp.float32),
             VMEM((length, 2 * length), jnp.int32),
-        ],
-        compiler_params=pltpu.CompilerParams(vmem_limit_bytes=60 * 2**20),
-    )(returned, node_index, node_slope, tables["z_backward"], tables["y_backward"])
+            VMEM((count, length, 2 * length), jnp.float32),
+            VMEM((length, 2 * length), jnp.float32),
+            VMEM(node_index.shape, jnp.float32),
+            pltpu.SemaphoreType.DMA((2, steps, grid_size)),
+            pltpu.SemaphoreType.DMA((2,)),
+        ]
+        + band_scratch(outer, steps, node_index.shape),
+        compiler_params=pltpu.CompilerParams(
+            collective_id=2, has_side_effects=True, vmem_limit_bytes=62 * 2**20
+        ),
+    )(
+        waves,
+        *shells,
+        table,
+        tables["x_forward"],
+        tables["x_backward"],
+        node_index,
+        node_slope,
+        tables["z_backward"],
+        tables["y_backward"],
+    )
 
 
 def fused_per_device(tables, partial_density, node_index, node_weight, node_slope, kernel_table):
@@ -816,8 +931,7 @@
     grid_size = lax.axis_size("grid")
     per = planes // grid_size
     band_at, grid_at = lax.axis_index("band"), lax.axis_index("grid")
-    density = band_sum(partial_density[0], 0)
-    waves = forward(density, node_index, node_weight, tables, count, planes, grid_size)
+    waves = forward(partial_density[0], node_index, node_weight, tables, count, planes, grid_size)
 
     full_range = jnp.arange(length, dtype=jnp.int32)
     own_planes = band_at * planes + grid_at * per + jnp.arange(per, dtype=jnp.int32)
@@ -833,11 +947,10 @@
     pair = jnp.concatenate([freq * freq, freq * freq + half * half])
     pair = jnp.pad(pair, (0, per * length - 2 * length))
     pair_shell, pair_frac = shell_split(jnp.stack([pair, pair + half * half]))
-    returned = middle(
-        waves, shell, frac, pair_shell, pair_frac, kernel_table, tables, planes, grid_size
-    )
-    potential = last(returned, node_index, node_slope, tables, count, planes)
-    return band_sum(potential, 3)
+    shells = (shell, frac, pair_shell, pair_frac)
+    return backward(
+        waves, shells, node_index, node_slope, kernel_table, tables, planes, grid_size
+    )
 
 
 def fits(mesh, length, groups):
@@ -849,7 +962,8 @@
         and planes % grids == 0
         and planes // grids >= 2
         and bands % 2 == 0
-        and (length // grids) % max(SUBLANES, bands) == 0
+        and bands == SUBLANES
+        and (length // grids) % SUBLANES == 0
     )
 
 

time: 392 us -> 253 us (0.65); the launches traced: 386 us -> 253 us
  Pallas kernels: 379 us -> 246 us
    pallas_call x5 -> x2, Pallas kernels: 379 us -> 246 us  [the longest x1 135 us: backward(): pl.pallas_call(lambda *refs: middle_kernel(sizes, *refs), in_specs=[whole...]
where the time goes in v2:
time: 253 us
  Pallas kernels  246 us (97%)
  local copies, waits for them, and re-layouts  4.1 us (2%)
  other arithmetic  3.07 us (1%)
    pallas_call x1, Pallas kernels, backward(): pl.pallas_call(lambda *refs: middle_kernel(sizes, *refs), in_specs=[whole...  135 us
    pallas_call x1, Pallas kernels, forward(): pl.pallas_call(lambda *refs: forward_kernel(sizes, *refs), in_specs=[whol...  111 us

profile of v2, /device:TPU:1, one launch (start us, length us, event | category | flops | bytes accessed | tf_op | source)
XLA Modules:
  0.0 252.9 jit_solution(6968659901495896503)
XLA Ops:
  0.1 0.1 fusion.9
  0.2 0.6 convert_subtract_fusion
  0.8 0.8 convert_add_fusion.refs_1_
  1.5 0.7 fusion.2.refs_2_
  2.3 1.0 pad.4
  3.3 0.8 pad_maximum_fusion.refs_5_
  4.1 110.9 %shard_map.109.refs_0_ = f32[2,2,16,160,128]{4,3,2,1,0:T(8,128)} custom-call(f32[32,128,128]{2,1,0:T(8,128)} %bitcast.11, s32[32,128,128]{2,1,0:T(8,128)} %refs_8_.1, f32[4,32,128,128]{3,2,1,0:T(8,128)} %refs_2_.1, bf16[8,32,256]{2,1,0:T(8,128)(2,1)} %constant.43.clone.refs_3_, bf16[2,768,256]{2,1,0:T(8,128)(2,1)} %constant.44.clone.refs_4_), custom_call_target="tpu_custom_call" | custom-call | tf_op jit(solution)/shard_map/pallas_call | solution.py:578
  115.0 134.8 %shard_map.110 = f32[32,128,128]{2,1,0:T(8,128)} custom-call(f32[2,2,16,160,128]{4,3,2,1,0:T(8,128)} %shard_map.109.refs_0_, s32[65,256]{1,0:T(8,128)} %convert_add_fusion.refs_1_, f32[65,256]{1,0:T(8,128)} %fusion.2.refs_2_, s32[2,256]{1,0:T(2,128)} %get-tuple-element.6.refs_3_, f32[2,256]{1,0:T(2,128)} %get-tuple-element.5.refs_4_, ...), custom_call_target="tpu_custom_call" | custom-call | tf_op jit(solution)/shard_map/pallas_call | solution.py:886
  249.8 3.1 %copy.13 = f32[32,128,128]{2,1,0:T(8,128)} copy(f32[32,128,128]{2,1,0:T(8,128)} %shard_map.110) | data formatting | bytes 4194304
  (9 shorter events, 0.1 us)

commit v3 on v0

--- a/solution.py
+++ b/solution.py
@@ -2,6 +2,7 @@
 
 import jax
 import jax.numpy as jnp
+import numpy as np
 from jax import lax
 from jax.experimental import pallas as pl
 from jax.experimental.pallas import tpu as pltpu
@@ -220,6 +221,726 @@
     return lax.psum(partial_potential, "band")
 
 
+LANES = 128
+SUBLANES = 8
+MESH = pl.DeviceIdType.MESH
+VMEM = pltpu.VMEM
+
+
+def split_table(table):
+    high = np.asarray(table).astype(jnp.bfloat16)
+    low = (np.asarray(table) - high.astype(np.float64)).astype(jnp.bfloat16)
+    return high, low
+
+
+def angles_of(sources, targets, length):
+    phase = (np.outer(sources, targets) % length) * (2.0 * np.pi / length)
+    return np.cos(phase), np.sin(phase)
+
+
+def complex_table(cosine, sine):
+    return np.stack([np.stack([cosine, -sine], 1), np.stack([sine, cosine], 1)])
+
+
+def constant_tables(length, bands, planes):
+    points = np.arange(length)
+    half = length // 2
+    cosine, sine = angles_of(points, points, length)
+    lower = ((points >= 1) & (points < half)).astype(np.float64)
+    upper = (points > half).astype(np.float64)
+    single = 1.0 - lower - upper
+    forward = complex_table(cosine, sine)
+    backward = complex_table(cosine, -sine)
+    packed = np.stack(
+        [
+            np.stack([cosine * (lower + single), -sine * lower], 1),
+            np.stack([cosine * upper, -sine * upper + cosine * single], 1),
+        ]
+    )
+    lo, up, one = (v[:, None] for v in (lower, upper, single))
+    opened = np.stack(
+        [
+            np.stack([cosine * (2 * lo + one), cosine * (2 * up)], 1),
+            np.stack([sine * (-2 * lo), sine * (-2 * up) + cosine * one], 1),
+        ]
+    )
+    square = (2 * length, 2 * length)
+
+    def right(table):
+        high, low = split_table(table.reshape(square))
+        return np.concatenate([high, low], 0)
+
+    def left(table):
+        high, low = split_table(table.reshape(square).T)
+        return np.concatenate([high, low], 1)
+
+    alternating = np.where(points % 2 == 0, 1.0, -1.0)
+    z_forward, z_backward = [], []
+    for band in range(bands):
+        ids = band * planes + np.arange(planes)
+        cos_z, sin_z = angles_of(ids, points, length)
+        minus = np.where(ids[:, None] == 0, alternating[None], -sin_z)
+        rows = np.concatenate([cos_z, minus], 0)
+        high, low = split_table(rows)
+        top = np.concatenate([high, high], 1)
+        bottom = np.concatenate([low, np.zeros_like(low)], 1)
+        z_forward.append(np.concatenate([top, bottom], 0))
+        first = ids[:, None] == 0
+        rows = np.concatenate(
+            [np.where(first, 1.0, 2.0 * cos_z), np.where(first, alternating[None], -2.0 * sin_z)]
+        ) / float(length) ** 3
+        high, low = split_table(rows.T)
+        z_backward.append(np.concatenate([high, low, high], 1))
+    return {
+        "y_forward": np.stack([right(packed), right(forward)]),
+        "y_backward": np.stack([right(opened), right(backward)]),
+        "x_forward": left(forward),
+        "x_backward": left(backward),
+        "z_forward": np.stack(z_forward),
+        "z_backward": np.stack(z_backward),
+    }
+
+
+def triple_left(values):
+    high, low = halves(values)
+    return jnp.concatenate([high, low, high], axis=1)
+
+
+def triple_right(values):
+    high, low = halves(values)
+    return jnp.concatenate([high, high, low], axis=0)
+
+
+def right_table(table):
+    high, low = table[: table.shape[0] // 2], table[table.shape[0] // 2 :]
+    return jnp.concatenate([high, high, low], axis=0)
+
+
+def left_table(table):
+    high, low = table[:, : table.shape[1] // 2], table[:, table.shape[1] // 2 :]
+    return jnp.concatenate([high, low, high], axis=1)
+
+
+def matmul(left, right):
+    return jnp.dot(left, right, preferred_element_type=jnp.float32)
+
+
+def matmul_nt(left, right):
+    return lax.dot_general(
+        left, right, (((1,), (1,)), ((), ())), preferred_element_type=jnp.float32
+    )
+
+
+def matmul_tn(left, right):
+    return lax.dot_general(
+        left, right, (((0,), (0,)), ((), ())), preferred_element_type=jnp.float32
+    )
+
+
+def greet(targets):
+    barrier = pltpu.get_barrier_semaphore()
+    for axis, target in targets:
+        pl.semaphore_signal(barrier, inc=1, device_id={axis: target}, device_id_type=MESH)
+    pl.semaphore_wait(barrier, len(targets))
+
+
+class BandSum:
+    def __init__(self, outer, chunk_rows, src, dst, near_buf, stage, far_buf, sems):
+        me = lax.axis_index("band")
+        self.outer, self.src, self.dst = outer, src, dst
+        self.near_buf, self.stage, self.far_buf, self.sems = near_buf, stage, far_buf, sems
+        self.far, self.near = me // 2, lax.rem(me, 2)
+        self.partner = self.far * 2 + (1 - self.near)
+        self.others = [lax.rem(self.far + 1 + j, outer) for j in range(outer)]
+        self.back = [lax.rem(self.far + outer - 1 - j, outer) for j in range(outer)]
+        self.chunk_rows = chunk_rows
+        self.side_rows = chunk_rows // 2
+        self.part = self.side_rows // outer
+        self.peers = [("band", self.partner)] + [
+            ("band", o * 2 + self.near) for o in self.others[:-1]
+        ]
+
+    def piece(self, chunk, side, quarter):
+        start = chunk * self.chunk_rows + side * self.side_rows + quarter * self.part
+        return pl.ds(start, self.part)
+
+    def copy(self, src, dst, chunk, kind, j, target):
+        return pltpu.make_async_remote_copy(
+            src_ref=src,
+            dst_ref=dst,
+            send_sem=self.sems.at[chunk, kind, 0, j],
+            recv_sem=self.sems.at[chunk, kind, 1, j],
+            device_id={"band": target},
+            device_id_type=MESH,
+        )
+
+    def near_copy(self, c, j):
+        src = self.src.at[self.piece(c, 1 - self.near, self.others[j])]
+        return self.copy(src, self.near_buf.at[c, j], c, 0, j, self.partner)
+
+    def far_copy(self, c, j):
+        target = self.others[j] * 2 + self.near
+        return self.copy(self.stage.at[c, j], self.far_buf.at[c, j], c, 1, j, target)
+
+    def gather_copy(self, c, j):
+        own = self.dst.at[self.piece(c, self.near, self.far)]
+        return self.copy(own, own, c, 2, j, self.others[j] * 2 + self.near)
+
+    def pass_copy(self, c, j):
+        block = self.dst.at[self.piece(c, self.near, self.back[j])]
+        return self.copy(block, block, c, 3, j, self.partner)
+
+    def start(self, c):
+        for j in range(self.outer):
+            self.near_copy(c, j).start()
+
+    def reduce(self, c):
+        for j in range(self.outer - 1):
+            self.near_copy(c, j).wait_recv()
+            mine = self.src[self.piece(c, self.near, self.others[j])]
+            self.stage[c, j] = mine + self.near_buf[c, j]
+            self.far_copy(c, j).start()
+
+    def finish(self, c):
+        last = self.outer - 1
+        self.near_copy(c, last).wait_recv()
+        own = self.piece(c, self.near, self.far)
+        total = self.src[own] + self.near_buf[c, last]
+        for j in range(last):
+            self.far_copy(c, j).wait_recv()
+            total = total + self.far_buf[c, j]
+        self.dst[own] = total
+        for j in range(last):
+            self.gather_copy(c, j).start()
+        self.pass_copy(c, last).start()
+
+    def forward(self, c):
+        for j in range(self.outer - 1):
+            self.gather_copy(c, j).wait_recv()
+            self.pass_copy(c, j).start()
+
+    def arrive(self, c):
+        for j in range(self.outer):
+            self.pass_copy(c, j).wait_recv()
+
+    def drain(self, c):
+        for j in range(self.outer):
+            self.near_copy(c, j).wait_send()
+            self.pass_copy(c, j).wait_send()
+        for j in range(self.outer - 1):
+            self.far_copy(c, j).wait_send()
+            self.gather_copy(c, j).wait_send()
+
+
+def whole_kernel(
+    sizes,
+    partial_hbm,
+    index_hbm,
+    weight_hbm,
+    slope_hbm,
+    table_ref,
+    tz_ref,
+    ty_ref,
+    tx_ref,
+    ti_ref,
+    bz_ref,
+    by_ref,
+    out_ref,
+    density_ref,
+    index_ref,
+    weight_ref,
+    theta,
+    columns,
+    ahead,
+    waves,
+    shells,
+    fracs,
+    spec,
+    mixed,
+    phi,
+    delta,
+    extra,
+    home,
+    back,
+    slab,
+    turned,
+    ids_ref,
+    fields,
+    total_ref,
+    ahead_sems,
+    home_sems,
+    load_sems,
+    near_buf,
+    stage,
+    far_buf,
+    density_sems,
+    potential_sems,
+):
+    count, padded, grid_size, planes, length, outer = sizes
+    per = planes // grid_size
+    grid_part = length // grid_size
+    steps = grid_part // SUBLANES
+    early = steps - 1
+    rows = count * SUBLANES
+    pitch = rows + SUBLANES
+    half = length // 2
+    pairs = half // 2 + 1
+    wide = 2 * length
+    band_at, me = lax.axis_index("band"), lax.axis_index("grid")
+    order = [lax.rem(me + 1 + j, grid_size) for j in range(grid_size)]
+    remote = range(grid_size - 1)
+    joint = (band_at == 0) & (me == 0)
+    buffers = (near_buf, stage, far_buf)
+    summed = BandSum(outer, SUBLANES, out_ref, density_ref, *buffers, density_sems)
+    result = BandSum(outer, SUBLANES, density_ref, out_ref, *buffers, potential_sems)
+
+    partial_load = pltpu.make_async_copy(partial_hbm, out_ref, load_sems.at[0])
+    index_load = pltpu.make_async_copy(index_hbm, index_ref, load_sems.at[1])
+    weight_load = pltpu.make_async_copy(weight_hbm, weight_ref, load_sems.at[2])
+    slope_load = pltpu.make_async_copy(slope_hbm, weight_ref, load_sems.at[3])
+    partial_load.start()
+    greet(summed.peers + [("grid", target) for target in order[:-1]])
+    partial_load.wait()
+    summed.start(0)
+    index_load.start()
+    weight_load.start()
+
+    def norms():
+        lane = lax.broadcasted_iota(jnp.int32, shells.shape[1:], 1)
+        row = lax.broadcasted_iota(jnp.int32, shells.shape[1:], 0)
+        side = (lane >= length).astype(jnp.int32)
+        ky = lane - side * length
+        fx, fy = frequency_of(2 * row + side, length), frequency_of(ky, length)
+        for k in range(per):
+            kz = band_at * planes + me * per + k
+            folded = jnp.where(ky > half, half * half, 0)
+            third = jnp.where(kz == 0, folded, kz * kz)
+            shells[k], fracs[k] = shell_split(fx * fx + fy * fy + third)
+        once = fy * fy + side * half * half
+        shells[per], fracs[per] = shell_split(once + row * half * half)
+
+    def ahead_copy(step, j, k):
+        return pltpu.make_async_remote_copy(
+            src_ref=ahead.at[step, j, k],
+            dst_ref=waves.at[k, :, me * steps + step],
+            send_sem=ahead_sems.at[0, step, j, k],
+            recv_sem=ahead_sems.at[1, step, j, k],
+            device_id={"grid": order[j]},
+            device_id_type=MESH,
+        )
+
+    def home_copy(step, j, k):
+        return pltpu.make_async_remote_copy(
+            src_ref=home.at[order[j], step, k],
+            dst_ref=back.at[step, me, k],
+            send_sem=home_sems.at[0, step, j, k],
+            recv_sem=home_sems.at[1, step, j, k],
+            device_id={"grid": order[j]},
+            device_id_type=MESH,
+        )
+
+    def own_copy(step):
+        sem = home_sems.at[0, step, grid_size - 1, 0]
+        return pltpu.make_async_copy(home.at[me, step], back.at[step, me], sem)
+
+    block = 32
+    half_rows = SUBLANES // 2
+
+    def fill(step, part):
+        def body(at, carry):
+            x_at = step * SUBLANES + part * half_rows + at // (length // block)
+            start = pl.multiple_of(lax.rem(at, length // block) * block, block)
+            place = pl.ds(pl.multiple_of(at * block, block), block)
+            index = index_ref[x_at, pl.ds(start, block), :] - 1
+            amount = density_ref[x_at, pl.ds(start, block), :]
+            parts = [amount * weight_ref[j, x_at, pl.ds(start, block), :] for j in range(4)]
+            for node in range(count):
+                value = jnp.where(index == node, parts[0], 0.0)
+                for j in range(1, 4):
+                    value = jnp.where(index == node - j, parts[j], value)
+                high, low = halves(value)
+                theta[node, place, 0:length] = high
+                theta[node, place, length:wide] = low
+            return carry
+
+        lax.fori_loop(0, half_rows * length // block, body, 0)
+
+    def columns_of(part):
+        table = tz_ref[band_at]
+
+        def body(node, carry):
+            for pair in range(half_rows // 2):
+                out = matmul_nt(table, theta[node, pair * wide : (pair + 1) * wide, :])
+                out = out[: 2 * planes] + out[2 * planes :]
+                for side in range(2):
+                    for c in range(2):
+                        row = c * planes * pitch + node * SUBLANES + part * half_rows
+                        columns[pl.ds(row + pair * 2 + side, planes, stride=pitch), :] = out[
+                            c * planes : (c + 1) * planes, side * length : (side + 1) * length
+                        ]
+            return carry
+
+        lax.fori_loop(0, count, body, 0)
+
+    def waves_of(step, j, k):
+        plane = order[j] * per + k
+        start = pl.multiple_of(plane * pitch, SUBLANES)
+        left = jnp.concatenate(
+            [columns[pl.ds(c * planes * pitch + start, rows), :] for c in range(2)], axis=1
+        )
+        kind = jnp.minimum(plane + band_at * planes, 1)
+        out = matmul(triple_left(left), right_table(ty_ref[kind]))
+        for d in range(2):
+            value = out[:, d * length : (d + 1) * length]
+            if j < grid_size - 1:
+                ahead[step, j, k, d] = value
+            else:
+                waves[k, d, me * steps + step] = value
+
+    def advance(call, chunk):
+        if chunk < steps:
+            call(chunk)
+
+    norms()
+    advance(summed.start, 1)
+    summed.reduce(0)
+    summed.finish(0)
+    advance(summed.reduce, 1)
+    summed.forward(0)
+    advance(summed.start, 2)
+    index_load.wait()
+    weight_load.wait()
+    for step in range(steps):
+        summed.arrive(step)
+        fill(step, 0)
+        columns_of(0)
+        advance(summed.finish, step + 1)
+        advance(summed.reduce, step + 2)
+        fill(step, 1)
+        columns_of(1)
+        advance(summed.forward, step + 1)
+        advance(summed.start, step + 3)
+        for k in range(per):
+            for j in range(grid_size):
+                waves_of(step, j, k)
+                if j < grid_size - 1 and (step < early or k < per - 1):
+                    ahead_copy(step, j, k).start()
+    for step in range(early, steps):
+        for j in remote:
+            ahead_copy(step, j, per - 1).start()
+    slope_load.start()
+    for step in range(steps):
+        summed.drain(step)
+
+    lane = lax.broadcasted_iota(jnp.int32, (16, length), 1)
+    slot = lax.broadcasted_iota(jnp.int32, (16, length), 0)
+    chosen = jnp.where((lane == slot * half) & (slot < 2), 1.0, 0.0).astype(jnp.bfloat16)
+    ids = lax.broadcasted_iota(jnp.int32, (table_ref.shape[1] // 3, wide), 0)
+
+    def hats(k, row):
+        shell, frac = shells[k, pl.ds(row, 1), :], fracs[k, pl.ds(row, 1), :]
+        return jnp.where(ids == shell, 1.0 - frac, jnp.where(ids == shell + 1, frac, 0.0))
+
+    def points_of(node, k, d):
+        start = node * SUBLANES
+        if not isinstance(node, int):
+            start = pl.multiple_of(start, SUBLANES)
+        return waves[k, d, :, pl.ds(start, SUBLANES), :].reshape(length, length)
+
+    def mix_rows(choices, load):
+        sums = [
+            [jnp.zeros((padded, length), jnp.float32) for _ in range(4)] for _ in range(choices)
+        ]
+        for node in range(count):
+            for tile in range(2):
+                part = phi[node * padded : (node + 1) * padded, tile * length : (tile + 1) * length]
+                for choice in range(choices):
+                    for e in range(2):
+                        value = part * load(node, e, choice, tile)
+                        sums[choice][2 * e + tile] = sums[choice][2 * e + tile] + value
+        return sums
+
+    def correction():
+        right = jnp.concatenate(
+            [tx_ref[:, length:wide], tx_ref[:, wide + length : 2 * wide]], axis=1
+        )
+
+        lines = []
+        for node in range(count):
+            high, low = halves(points_of(node, 0, 1))
+            lines.append((matmul_nt(chosen, high) + matmul_nt(chosen, low))[:SUBLANES])
+        high, low = halves(-2.0 * jnp.concatenate(lines, axis=0))
+        both = jnp.concatenate([high, high], axis=1)
+        out = matmul_nt(both, right)
+        low = jnp.concatenate([low, jnp.zeros_like(low)], axis=1)
+        out = out + matmul_nt(low, right)
+        delta[...] = out.reshape(count, SUBLANES, wide)
+        phi[...] = matmul(table_ref[...], triple_right(0.5 * (hats(per, 0) - hats(per, 1))))
+        sums = mix_rows(
+            1,
+            lambda node, e, choice, tile: delta[
+                node, tile : tile + 1, e * length : (e + 1) * length
+            ],
+        )[0]
+        inverse = jnp.concatenate(
+            [ti_ref[:, 0:wide], ti_ref[:, 0:wide], ti_ref[:, wide : 2 * wide]], axis=1
+        )
+        for r in range(2):
+            left = jnp.concatenate([sums[r], sums[2 + r]], axis=1)
+            added = matmul_nt(triple_left(left), inverse)
+            for c in range(2):
+                value = added[:, c * length : (c + 1) * length]
+                extra[c, pl.ds(r, padded, stride=SUBLANES), :] = value
+
+    def middle(k):
+        for step in range(steps):
+            for j in remote:
+                ahead_copy(step, j, k).wait_recv()
+
+        def to_spectrum(pair, carry):
+            values = jnp.concatenate(
+                [
+                    jnp.concatenate([points_of(2 * pair + side, k, d) for side in range(2)], axis=1)
+                    for d in range(2)
+                ],
+                axis=0,
+            )
+            out = matmul(left_table(tx_ref[...]), triple_right(values))
+            for side in range(2):
+                spec[2 * pair + side] = out[:, side * length : (side + 1) * length]
+            return carry
+
+        lax.fori_loop(0, count // 2, to_spectrum, 0)
+
+        def mix_pair(t, carry):
+            phi[...] = matmul(table_ref[...], triple_right(hats(k, t)))
+            at = [[2 * t, 2 * t + 1]]
+            at.append([lax.rem(length - i, length) for i in at[0]])
+            sums = mix_rows(
+                2,
+                lambda node, e, choice, tile: spec[
+                    node, pl.ds(e * length + at[choice][tile], 1), :
+                ],
+            )
+            for choice in range(2):
+                for e in range(2):
+                    for tile in range(2):
+                        start = (e * length + at[choice][tile]) * padded
+                        place = pl.ds(pl.multiple_of(start, SUBLANES), padded)
+                        mixed[place, :] = sums[choice][2 * e + tile]
+            return carry
+
+        lax.fori_loop(0, pairs, mix_pair, 0)
+        if k == 0:
+            extra[...] = jnp.zeros_like(extra)
+            pl.when(joint)(correction)
+
+        def to_slabs(pair, carry):
+            nodes = [2 * pair + side for side in range(2)]
+            lines = [mixed[pl.ds(node, wide, stride=padded), :] for node in nodes]
+            out = matmul(left_table(ti_ref[...]), triple_right(jnp.concatenate(lines, axis=1)))
+            for side, node in enumerate(nodes):
+                place = pl.ds(pl.multiple_of(node * SUBLANES, SUBLANES), SUBLANES)
+                value = out[:, side * length : (side + 1) * length]
+                if k == 0:
+                    line = jnp.concatenate([extra[c, place, :] for c in range(2)], axis=1)
+                    both = jnp.concatenate(halves(line), axis=0)
+                    mask = jnp.concatenate([chosen[:SUBLANES], chosen[:SUBLANES]], axis=0)
+                    value = value + matmul_tn(both, mask)
+                for c in range(2):
+                    part = value[c * length : (c + 1) * length]
+                    part = part.reshape(grid_size, steps, SUBLANES, length)
+                    home[:, :, k, c, place, :] = part
+            return carry
+
+        lax.fori_loop(0, count // 2, to_slabs, 0)
+
+    for k in range(per):
+        middle(k)
+        for step in range(early):
+            for j in remote:
+                home_copy(step, j, k).start()
+    for step in range(early, steps):
+        for k in range(per):
+            for j in remote:
+                home_copy(step, j, k).start()
+    for step in range(steps):
+        own_copy(step).start()
+    slope_load.wait()
+    table = bz_ref[band_at]
+
+    def y_rows(step):
+        def body(plane, carry):
+            kind = jnp.minimum(plane + band_at * planes, 1)
+            left = jnp.concatenate(
+                [back[step, plane // per, lax.rem(plane, per), c] for c in range(2)], axis=1
+            )
+            out = matmul(triple_left(left), right_table(by_ref[kind]))
+            for c in range(2):
+                start = pl.multiple_of((c * planes + plane) * pitch, SUBLANES)
+                slab[pl.ds(start, rows), :] = out[:, c * length : (c + 1) * length]
+            return carry
+
+        lax.fori_loop(0, planes, body, 0)
+
+    def z_rows(step):
+        def pair_of(pair, carry):
+            first = step * SUBLANES + pair * 2
+            for side in range(2):
+                lanes = slice(side * length, (side + 1) * length)
+                ids_ref[:, lanes] = index_ref[first + side].T - 1
+                for j in range(4):
+                    turned[j, :, lanes] = weight_ref[j, first + side].T
+            for node in range(count):
+                sides = []
+                for side in range(2):
+                    start = node * SUBLANES + pair * 2 + side
+                    parts = [
+                        slab[pl.ds(c * planes * pitch + start, planes, stride=pitch), :]
+                        for c in range(2)
+                    ]
+                    sides.append(jnp.concatenate(parts, axis=0))
+                fields[node] = matmul(table, triple_right(jnp.concatenate(sides, axis=1)))
+
+            def pick(block, carry):
+                place = pl.ds(pl.multiple_of(block * SUBLANES, SUBLANES), SUBLANES)
+                index = ids_ref[place, :]
+                picked = [jnp.zeros((SUBLANES, wide), jnp.float32) for _ in range(4)]
+                for node in range(count):
+                    field = fields[node, place, :]
+                    for j in range(4):
+                        picked[j] = jnp.where(index == node - j, field, picked[j])
+                summed = picked[0] * turned[0, place, :]
+                for j in range(1, 4):
+                    summed = summed + picked[j] * turned[j, place, :]
+                total_ref[place, :] = summed
+                return carry
+
+            lax.fori_loop(0, length // SUBLANES, pick, 0)
+            for side in range(2):
+                lanes = slice(side * length, (side + 1) * length)
+                density_ref[first + side] = total_ref[:, lanes].T
+            return carry
+
+        lax.fori_loop(0, SUBLANES // 2, pair_of, 0)
+
+    for at in range(steps):
+        own_copy(at).wait()
+        for j in remote:
+            for k in range(per):
+                home_copy(at, j, k).wait_recv()
+        y_rows(at)
+        z_rows(at)
+        result.start(at)
+        if at > 0:
+            result.finish(at - 1)
+        result.reduce(at)
+        if at > 0:
+            result.forward(at - 1)
+    result.finish(steps - 1)
+    result.forward(steps - 1)
+    for step in range(steps):
+        result.arrive(step)
+        result.drain(step)
+        for j in remote:
+            for k in range(per):
+                ahead_copy(step, j, k).wait_send()
+                home_copy(step, j, k).wait_send()
+
+
+def fused_per_device(tables, partial_density, node_index, node_weight, node_slope, kernel_table):
+    grid_part, length = node_index.shape[:2]
+    count = kernel_table.shape[0]
+    planes = length // 2 // lax.axis_size("band")
+    grid_size = lax.axis_size("grid")
+    outer = lax.axis_size("band") // 2
+    per = planes // grid_size
+    steps = grid_part // SUBLANES
+    rows = count * SUBLANES
+    wide = 2 * length
+    padded = -(-count // SUBLANES) * SUBLANES
+    depth = -(-(kernel_table.shape[2]) // LANES) * LANES
+    table = jnp.pad(kernel_table, ((0, 0), (0, padded - count), (0, depth - kernel_table.shape[2])))
+    table = table.reshape(count * padded, depth)
+    rounded = lax.reduce_precision(table, exponent_bits=8, mantissa_bits=7)
+    high, low = rounded.astype(jnp.bfloat16), (table - rounded).astype(jnp.bfloat16)
+    table = jnp.concatenate([high, low, high], axis=1)
+    sizes = (count, padded, grid_size, planes, length, outer)
+    pairs = -(-(length // 4 + 1) // SUBLANES) * SUBLANES
+    piece = (SUBLANES // (2 * outer), length, length)
+    floats = lambda *shape: VMEM(shape, jnp.float32)
+    dma = lambda *shape: pltpu.SemaphoreType.DMA(shape)
+    whole = pl.BlockSpec(memory_space=VMEM)
+    anywhere = pl.BlockSpec(memory_space=pl.ANY)
+    return pl.pallas_call(
+        lambda *refs: whole_kernel(sizes, *refs),
+        in_specs=[anywhere] * 4 + [whole] * 7,
+        out_specs=whole,
+        out_shape=jax.ShapeDtypeStruct(node_index.shape, jnp.float32),
+        scratch_shapes=[
+            floats(*node_index.shape),
+            VMEM(node_index.shape, jnp.int32),
+            floats(*node_weight.shape),
+            VMEM((count, SUBLANES // 2 * length, wide), jnp.bfloat16),
+            floats(2 * planes * (rows + SUBLANES), length),
+            floats(steps, grid_size - 1, per, 2, rows, length),
+            floats(per, 2, grid_size * steps, rows, length),
+            VMEM((per + 1, pairs, wide), jnp.int32),
+            floats(per + 1, pairs, wide),
+            floats(count, wide, length),
+            floats(wide * padded, length),
+            floats(count * padded, wide),
+            floats(count, SUBLANES, wide),
+            floats(2, padded * SUBLANES, length),
+            floats(grid_size, steps, per, 2, rows, length),
+            floats(steps, grid_size, per, 2, rows, length),
+            floats(2 * planes * (rows + SUBLANES), length),
+            floats(4, length, wide),
+            VMEM((length, wide), jnp.int32),
+            floats(count, length, wide),
+            floats(length, wide),
+            dma(2, steps, grid_size - 1, per),
+            dma(2, steps, grid_size, per),
+            dma(4),
+            floats(steps, outer, *piece),
+            floats(steps, outer - 1, *piece),
+            floats(steps, outer - 1, *piece),
+            dma(steps, 4, 2, outer),
+            dma(steps, 4, 2, outer),
+        ],
+        compiler_params=pltpu.CompilerParams(
+            collective_id=1, has_side_effects=True, vmem_limit_bytes=67043328
+        ),
+    )(
+        partial_density[0],
+        node_index,
+        node_weight,
+        node_slope,
+        table,
+        tables["z_forward"],
+        tables["y_forward"],
+        tables["x_forward"],
+        tables["x_backward"],
+        tables["z_backward"],
+        tables["y_backward"],
+    )
+
+
+def fits(mesh, length, count):
+    bands, grids = mesh.shape["band"], mesh.shape["grid"]
+    planes = length // 2 // bands
+    return (
+        length == LANES
+        and planes == SUBLANES
+        and planes % grids == 0
+        and planes // grids >= 2
+        and bands % 2 == 0
+        and bands == SUBLANES
+        and count % 2 == 0
+        and (length // grids) % SUBLANES == 0
+    )
+
+
 def solution(mesh):
     placed = (
         P("band", "grid", None, None),
@@ -228,6 +949,17 @@
         P(None, "grid", None, None),
         P(),
     )
-    return jax.shard_map(
-        per_device, mesh=mesh, in_specs=placed, out_specs=P("grid", None, None), check_vma=False
-    )
+
+    def program(*args):
+        length = args[1].shape[0]
+        body = per_device
+        if fits(mesh, length, args[4].shape[0]):
+            bands = mesh.shape["band"]
+            tables = constant_tables(length, bands, length // 2 // bands)
+            tables = {name: jnp.asarray(table) for name, table in tables.items()}
+            body = lambda *blocks: fused_per_device(tables, *blocks)
+        return jax.shard_map(
+            body, mesh=mesh, in_specs=placed, out_specs=P("grid", None, None), check_vma=False
+        )(*args)
+
+    return program

time: 761 us -> 219 us (0.29); the launches traced: 750 us -> 219 us
  waiting for transfers between devices: 306 us -> 0 us
  Pallas kernels: 40.6 us -> 214 us
  matrix products: 161 us -> 0 us
  local copies, waits for them, and re-layouts: 158 us -> 4.1 us
  other arithmetic: 46.6 us -> 0.82 us
  starting transfers between devices: 23.1 us -> 0 us
  between operations: 14 us -> 0.02 us
    psum x2 -> x0, waiting for transfers between devices: 200 us -> none  [the longest x1 101 us: per_device(): return lax.psum(partial_potential, 'band')]
    pallas_call x1, Pallas kernels: 40.6 us -> 214 us  [fused_per_device(): pl.pallas_call(lambda *refs: whole_kernel(sizes, *refs), in_specs=[anywhe...]
    dot_general x7 -> x0, matrix products: 161 us -> none  [the longest x6 161 us: short(): return jnp.einsum(pattern, left, right, precision=lax.Precision.HIGH)]
    all_to_all x2 -> x0, waiting for transfers between devices: 105 us -> none  [the longest x1 54.2 us: per_device(): lax.all_to_all(waves, 'grid', split_axis=0, concat_axis=0, tiled=True)]
    unnamed x20 -> x1, local copies, waits for them, and re-layouts: 86.5 us -> 3.14 us
    reshape x2 -> x0, local copies, waits for them, and re-layouts: 39.4 us -> none  [per_device(): waves = waves.reshape((grid_size, grid_part) + waves.shape[1:])]
    all_to_all x2 -> x0, other arithmetic: 35.9 us -> none  [the longest x1 18 us: per_device(): lax.all_to_all(inverse, 'grid', split_axis=0, concat_axis=0, tiled=True)]
    all_to_all x2 -> x0, starting transfers between devices: 23.1 us -> none  [the longest x1 17 us: per_device(): lax.all_to_all(waves, 'grid', split_axis=0, concat_axis=0, tiled=True)]
  transfers between devices with their start and end apart: 4 -> 0, of which waited for: 4 -> 0; matrix products, arithmetic and copies ran while one was open for 3% -> 0% of each run, Pallas kernels for 0% -> 0%
where the time goes in v3:
time: 219 us
  Pallas kernels  214 us (98%)
  local copies, waits for them, and re-layouts  4.1 us (2%)
    pallas_call x1, Pallas kernels, fused_per_device(): pl.pallas_call(lambda *refs: whole_kernel(sizes, *refs), in_specs=[anywhe...  214 us

profile of v3, /device:TPU:1, one launch (start us, length us, event | category | flops | bytes accessed | tf_op | source)
XLA Modules:
  0.0 218.9 jit_solution(14481632908799533732)
XLA Ops:
  0.0 1.0 pad.4
  1.0 0.8 pad_maximum_fusion.refs_4_
  1.8 214.0 %shard_map.109 = f32[32,128,128]{2,1,0:T(8,128)} custom-call(f32[32,128,128]{2,1,0:T(8,128)} %bitcast.4, s32[32,128,128]{2,1,0:T(8,128)} %refs_1_.1, f32[4,32,128,128]{3,2,1,0:T(8,128)} %refs_2_.1, f32[4,32,128,128]{3,2,1,0:T(8,128)} %refs_3_.1, bf16[480,384]{1,0:T(8,128)(2,1)} %pad_maximum_fusion.refs_4_, bf16[8,32,256]{2,1,0:T(8,128)(2,1)} %constant.15.clone.refs_5_, ...), custom_call_target="tpu_custom_call" | custom-call | tf_op jit(solution)/shard_map/pallas_call | solution.py:875
  215.8 3.1 %copy.13 = f32[32,128,128]{2,1,0:T(8,128)} copy(f32[32,128,128]{2,1,0:T(8,128)} %shard_map.109) | data formatting | bytes 4194304
  (1 shorter events, 0.0 us)

commit v4 on v3

--- a/solution.py
+++ b/solution.py
@@ -458,6 +458,7 @@
     spec,
     mixed,
     phi,
+    other,
     delta,
     extra,
     home,
@@ -612,13 +613,13 @@
     weight_load.wait()
     for step in range(steps):
         summed.arrive(step)
+        advance(summed.finish, step + 1)
         fill(step, 0)
         columns_of(0)
-        advance(summed.finish, step + 1)
         advance(summed.reduce, step + 2)
+        advance(summed.forward, step + 1)
         fill(step, 1)
         columns_of(1)
-        advance(summed.forward, step + 1)
         advance(summed.start, step + 3)
         for k in range(per):
             for j in range(grid_size):
@@ -647,7 +648,7 @@
             start = pl.multiple_of(start, SUBLANES)
         return waves[k, d, :, pl.ds(start, SUBLANES), :].reshape(length, length)
 
-    def mix_rows(choices, load):
+    def mix_rows(phi, choices, load):
         sums = [
             [jnp.zeros((padded, length), jnp.float32) for _ in range(4)] for _ in range(choices)
         ]
@@ -677,6 +678,7 @@
         delta[...] = out.reshape(count, SUBLANES, wide)
         phi[...] = matmul(table_ref[...], triple_right(0.5 * (hats(per, 0) - hats(per, 1))))
         sums = mix_rows(
+            phi,
             1,
             lambda node, e, choice, tile: delta[
                 node, tile : tile + 1, e * length : (e + 1) * length
@@ -712,11 +714,11 @@
 
         lax.fori_loop(0, count // 2, to_spectrum, 0)
 
-        def mix_pair(t, carry):
-            phi[...] = matmul(table_ref[...], triple_right(hats(k, t)))
+        def mix_pair(phi, t):
             at = [[2 * t, 2 * t + 1]]
             at.append([lax.rem(length - i, length) for i in at[0]])
             sums = mix_rows(
+                phi,
                 2,
                 lambda node, e, choice, tile: spec[
                     node, pl.ds(e * length + at[choice][tile], 1), :
@@ -728,9 +730,20 @@
                         start = (e * length + at[choice][tile]) * padded
                         place = pl.ds(pl.multiple_of(start, SUBLANES), padded)
                         mixed[place, :] = sums[choice][2 * e + tile]
+
+        def weigh(target, t):
+            target[...] = matmul(table_ref[...], triple_right(hats(k, t)))
+
+        def mix_two(i, carry):
+            weigh(other, 2 * i + 1)
+            mix_pair(phi, 2 * i)
+            weigh(phi, 2 * i + 2)
+            mix_pair(other, 2 * i + 1)
             return carry
 
-        lax.fori_loop(0, pairs, mix_pair, 0)
+        weigh(phi, 0)
+        lax.fori_loop(0, pairs // 2, mix_two, 0)
+        mix_pair(phi, pairs - 1)
         if k == 0:
             extra[...] = jnp.zeros_like(extra)
             pl.when(joint)(correction)
@@ -890,6 +903,7 @@
             floats(count, wide, length),
             floats(wide * padded, length),
             floats(count * padded, wide),
+            floats(count * padded, wide),
             floats(count, SUBLANES, wide),
             floats(2, padded * SUBLANES, length),
             floats(grid_size, steps, per, 2, rows, length),
@@ -937,6 +951,7 @@
         and bands % 2 == 0
         and bands == SUBLANES
         and count % 2 == 0
+        and (length // 4) % 2 == 0
         and (length // grids) % SUBLANES == 0
     )
 

time: 219 us -> 216 us (0.986)
  Pallas kernels: 214 us -> 211 us
    pallas_call x1, Pallas kernels: 214 us -> 211 us  [fused_per_device(): pl.pallas_call(lambda *refs: whole_kernel(sizes, *refs), in_specs=[anywhe...]
where the time goes in v4:
time: 216 us; the launch traced here: 215 us
  Pallas kernels  211 us (98%)
  local copies, waits for them, and re-layouts  4.1 us (2%)
    pallas_call x1, Pallas kernels, fused_per_device(): pl.pallas_call(lambda *refs: whole_kernel(sizes, *refs), in_specs=[anywhe...  211 us

profile of v4, /device:TPU:1, one launch (start us, length us, event | category | flops | bytes accessed | tf_op | source)
XLA Modules:
  0.0 215.5 jit_solution(8326705118262120862)
XLA Ops:
  0.0 1.0 pad.4
  1.0 0.8 pad_maximum_fusion.refs_4_
  1.8 210.5 %shard_map.109 = f32[32,128,128]{2,1,0:T(8,128)} custom-call(f32[32,128,128]{2,1,0:T(8,128)} %bitcast.4, s32[32,128,128]{2,1,0:T(8,128)} %refs_1_.1, f32[4,32,128,128]{3,2,1,0:T(8,128)} %refs_2_.1, f32[4,32,128,128]{3,2,1,0:T(8,128)} %refs_3_.1, bf16[480,384]{1,0:T(8,128)(2,1)} %pad_maximum_fusion.refs_4_, bf16[8,32,256]{2,1,0:T(8,128)(2,1)} %constant.15.clone.refs_5_, ...), custom_call_target="tpu_custom_call" | custom-call | tf_op jit(solution)/shard_map/pallas_call | solution.py:888
  212.3 3.1 %copy.13 = f32[32,128,128]{2,1,0:T(8,128)} copy(f32[32,128,128]{2,1,0:T(8,128)} %shard_map.109) | data formatting | bytes 4194304
  (1 shorter events, 0.0 us)
